TPU v7x, 128 devices: a whole 4x4x4 slice. The times are simulated.
128 devices in a mesh: tile: 8 (over y, core), slab: 16 (over z, x).
Axes of the slice: x: 4, y: 4, z: 4, core: 2. Of those that a mesh axis runs over, the one named last changes fastest.
Arguments:
- volume: float32 [512, 32768], P('slab', 'tile'), may hold values from -6 to 6
- measured: float32 [512, 8192], P('slab', 'tile'), may hold values from -6 to 6
- weights: float32 [512, 8192], P('slab', 'tile'), may hold values from 0.25 to 4
- footprints: float32 [2048, 32, 128], P('tile'), may hold values from -0.1875 to 0.1875
- foot_pixel: int32 [2048], P('tile'), may hold values from 0 to 31
- foot_strip: int32 [2048], P('tile'), may hold values from 0 to 255
Outputs:
- smoothed: float32 [512, 32768], P('slab', 'tile')
- residual: float32 [512, 8192], P('slab', 'tile')
Inputs may be any that keep to these rules, and one draw needn't show every extreme that they name: foot_pixel names one of the 32 pixel blocks of the tile that holds the footprint block. foot_strip names a strip of 32 rays.
All inputs are finite; a program needn't handle non-finite values.
Results may differ from a plain program's by a relative error of at most 0.0003.
Values sent between devices are 32-bit elements; how exact they have to be, the bound alone decides.
No kernel may reach another device: no remote copies, remote signals or barrier semaphores. Data moves between devices by JAX's collectives and lax.ppermute only.
A program may use at most 64 MiB of HBM per device.

v0:
```python
import jax
import jax.numpy as jnp
from jax import lax
from jax.experimental import pallas as pl
from jax.experimental.pallas import tpu as pltpu
from jax.sharding import Mesh
from jax.sharding import PartitionSpec as P


PASSES = 3
TILE = ("tile_0", "tile_1")
SLAB = ("slab_0", "slab_1")
GROUP = 4
UNROLL = 64
CHUNKS = 4

huber_width = 0.5
smooth_rate = 0.2


VM = pl.BlockSpec(memory_space=pltpu.VMEM)
SM = pl.BlockSpec(memory_space=pltpu.SMEM)
AN = pl.BlockSpec(memory_space=pltpu.HBM)
F32 = jnp.float32
BF16 = jnp.bfloat16


def call(kernel, outs, ins, scratch=(), smem=0, flops=1000000, limit=10, any_at=()):
    specs = [AN if n in any_at else SM if n < smem else VM for n in range(len(ins))]
    return pl.pallas_call(
        kernel,
        out_shape=[s if hasattr(s, "dtype") else jax.ShapeDtypeStruct(s, F32) for s in outs],
        in_specs=specs,
        out_specs=[VM] * len(outs),
        scratch_shapes=list(scratch),
        compiler_params=pltpu.CompilerParams(vmem_limit_bytes=limit << 20),
        cost_estimate=pl.CostEstimate(flops=flops, bytes_accessed=1 << 20, transcendentals=0),
    )(*ins)


def halves(value):
    high = value.astype(BF16)
    return high, (value - high.astype(F32)).astype(BF16)


def lane_groups(shape):
    return lax.broadcasted_iota(jnp.int32, shape, 1) // 32


def place(spots, b):
    pixels, strips, me = spots
    strip = strips[b]
    owner = strip >> 5
    slot = (((owner & 1) ^ me[1]) << 2) | (((owner >> 1) - me[0]) & 3)
    return (slot << 3) | ((strip >> 2) & 7), strip & 3, pixels[b]


def stacked(pair):
    high = pair[:, :128]
    return jnp.concatenate([pair, jnp.concatenate([high, jnp.zeros_like(high)], axis=1)], axis=0)


def forward_step(spots, g, pair, high, low, rays, groups):
    where = [place(spots, GROUP * g + i) for i in range(GROUP)]
    left = jnp.concatenate([jnp.concatenate([high[w[2]], low[w[2]]], axis=1) for w in where], axis=0)
    both = lax.dot_general(left, stacked(pair), (((1,), (0,)), ((), ())), preferred_element_type=F32)
    product = both[:, :128] + both[:, 128:]
    for i, (entry, spot, _) in enumerate(where):
        own = jnp.where(groups == i, product[32 * i : 32 * i + 32], 0.0)
        rays[entry] += pltpu.roll(own, ((spot - i) & 3) * 32, 1)


def forward_loop(spots, turned, high, low, rays):
    rays[...] = jnp.zeros_like(rays)
    groups = lane_groups((32, 128))

    def step(g, carry):
        forward_step(spots, g, turned[g], high, low, rays, groups)
        return carry

    lax.fori_loop(0, turned.shape[0], step, 0, unroll=UNROLL)


def back_loop(spots, plain, rays, field):
    field[...] = jnp.zeros_like(field)
    groups = lane_groups((32, 128))

    def step(g, carry):
        where = [place(spots, GROUP * g + i) for i in range(GROUP)]
        rows = []
        for i, (entry, spot, _) in enumerate(where):
            turned = pltpu.roll(rays[entry], ((i - spot) & 3) * 32, 1)
            own = jnp.where(groups == i, turned, 0.0)
            rows.append(jnp.concatenate(halves(own), axis=1))
        left = jnp.concatenate(rows, axis=0)
        both = lax.dot_general(
            left, stacked(plain[g]), (((1,), (0,)), ((), ())), preferred_element_type=F32
        )
        product = both[:, :128] + both[:, 128:]
        for i, (_, _, pixel) in enumerate(where):
            field[pixel] += product[32 * i : 32 * i + 32]
        return carry

    lax.fori_loop(0, plain.shape[0], step, 0, unroll=UNROLL)


def hand_out(rays, mine, theirs):
    mine[...] = rays[:32].reshape(mine.shape)
    theirs[...] = rays[32:].reshape(theirs.shape)


def first_kernel(pixels_hbm, strips_hbm, me, foot_hbm, volume_hbm, *refs):
    mine, theirs, first, last, plain, turned, foot, volume, high, low, rays, pixels, strips, sem, foot_sem = refs
    spots = (pixels, strips, me)
    per = foot.shape[0] // CHUNKS

    def chunk(t):
        some = pl.ds(t * per, per)
        return pltpu.make_async_copy(foot_hbm.at[some], foot.at[some], foot_sem.at[t])

    field = pltpu.make_async_copy(volume_hbm, volume, sem.at[0])
    field.start()
    indices = [
        pltpu.make_async_copy(pixels_hbm, pixels, sem.at[1]),
        pltpu.make_async_copy(strips_hbm, strips, sem.at[2]),
    ]
    for copy in indices:
        copy.start()
    for t in range(CHUNKS):
        chunk(t).start()
    rays[...] = jnp.zeros_like(rays)
    groups = lane_groups((32, 128))
    for copy in (*indices, field):
        copy.wait()
    for p in range(high.shape[0]):
        cols = slice(128 * p, 128 * p + 128)
        high[p], low[p] = halves(volume[:, cols])
        first[p], last[p] = volume[0:8, cols], volume[24:32, cols]

    def trip(t, carry):
        chunk(t).wait()
        for u in range(per // GROUP):
            g = t * (per // GROUP) + u
            block = foot[pl.ds(GROUP * g, GROUP)].reshape(GROUP * 32, 128)
            plain[g] = jnp.concatenate(halves(block), axis=1)
            pair = jnp.concatenate(halves(block.T), axis=1)
            turned[g] = pair
            forward_step(spots, g, pair, high, low, rays, groups)
        return carry

    lax.fori_loop(0, CHUNKS, trip, 0)
    hand_out(rays, mine, theirs)


def folded(value):
    return jnp.sum(value.reshape(-1, 8, 128), axis=0)


def there_and_back(spots, plain, turned, pieces, mine, theirs, field, high, low, rays):
    for slot, piece in enumerate(pieces):
        rays[8 * slot : 8 * slot + 8] = piece[...]
    back_loop(spots, plain, rays, field)
    for p in range(high.shape[0]):
        high[p], low[p] = halves(field[p])
    forward_loop(spots, turned, high, low, rays)
    hand_out(rays, mine, theirs)


def two_firsts(one, other):
    row = lax.broadcasted_iota(jnp.int32, (8, 128), 0)
    return jnp.where(row < 3, one, pltpu.roll(other, 3, 0))


def two_lasts(one, other):
    row = lax.broadcasted_iota(jnp.int32, (8, 128), 0)
    return jnp.where(row > 4, one, pltpu.roll(other, 5, 0))


def second_kernel(pixels, strips, me, plain, turned, *refs):
    pieces, first0, last0 = refs[:8], refs[8], refs[9]
    mine, theirs, field, sums, first, last, high, low, rays = refs[10:]
    there_and_back((pixels, strips, me), plain, turned, pieces, mine, theirs, field, high, low, rays)
    sums[0] = folded(field[...] * field[...])
    for p in range(field.shape[0]):
        first[p] = two_firsts(first0[p], field[p, 0:8])
        last[p] = two_lasts(last0[p], field[p, 24:32])


def third_kernel(pixels, strips, me, plain, turned, *refs):
    pieces, grad = refs[:8], refs[8]
    mine, theirs, field, sums, first, last, high, low, rays = refs[9:]
    there_and_back((pixels, strips, me), plain, turned, pieces, mine, theirs, field, high, low, rays)
    sums[0] = folded(grad[...] * field[...])
    sums[1] = folded(field[...] * field[...])
    for q in range(first.shape[0]):
        one, other = field[2 * q], field[2 * q + 1]
        first[q] = two_firsts(one[0:8], other[0:8])
        last[q] = two_lasts(one[24:32], other[24:32])


def add_kernel(mine, got, kept, s1, s2, s3):
    for r, out in enumerate((kept, s1, s2, s3)):
        out[...] = mine[r] + got[r]


def tile_cols(ref):
    return jnp.stack([ref[:, 128 * t : 128 * t + 128] for t in range(ref.shape[1] // 128)])


def start_kernel(kept, a, b, c, measured, weights, residual, sent):
    value = kept[...] + a[...] + b[...] + c[...] - tile_cols(measured)
    residual[...] = value
    sent[...] = tile_cols(weights) * value


def resend_kernel(kept, a, b, c, weights, sent):
    sent[...] = tile_cols(weights) * (kept[...] + a[...] + b[...] + c[...])


def middle_kernel(kept, a, b, c, sent, back, projected, sums, spare):
    spare[...] = back[...]
    value = kept[...] + a[...] + b[...] + c[...]
    projected[...] = value
    sums[0] = folded(sent[...] * value)


SPAN = 16


def in_lanes(sums, shape):
    rows = [jnp.sum(part, axis=0, keepdims=True) for part in sums]
    rows += [jnp.zeros((1, 128), F32)] * (8 - len(rows))
    value = jnp.concatenate(rows, axis=0)
    for by in (64, 32, 16):
        value = value + pltpu.roll(value, by, 1)
    own = lax.broadcasted_iota(jnp.int32, (8, 128), 0) == lax.broadcasted_iota(jnp.int32, (8, 128), 1) // SPAN
    return jnp.broadcast_to(jnp.sum(jnp.where(own, value, 0.0), axis=0, keepdims=True), shape)


def end_kernel(kept, a, b, c, weights, before, norm0, curve0, turned, projected, rows):
    value = kept[...] + a[...] + b[...] + c[...]
    weighted = tile_cols(weights) * value
    projected[...] = value
    cross = folded(weighted * before[...])
    rows[...] = in_lanes([norm0[0], curve0[0], turned[0], turned[1], cross, folded(weighted * value)], rows.shape)


def totals(rows, count):
    value = jnp.sum(rows[...], axis=0, keepdims=True)
    group = lax.broadcasted_iota(jnp.int32, value.shape, 1) // SPAN
    return [jnp.sum(jnp.where(group == n, value, 0.0), axis=1, keepdims=True) for n in range(count)]


def scalar(value):
    return jnp.sum(value)


def judge_kernel(rows, alphas, again):
    norm0, curve0, cross_g, square_g, cross_p, square_p = totals(rows, 6)
    alpha = norm0 / curve0
    norm1 = norm0 - 2.0 * alpha * cross_g + alpha * alpha * square_g
    curve1 = curve0 - 2.0 * alpha * cross_p + alpha * alpha * square_p
    sound = (norm1 > 0.01 * norm0) & (curve1 > 0.01 * curve0)
    for square in (square_g, square_p):
        sound = sound & (square > 1e-25) & (square < 1e37)
    alphas[0] = scalar(alpha)
    alphas[1] = scalar(norm1 / curve1)
    again[0] = jnp.where(scalar(jnp.where(sound, F32(0.0), F32(1.0))) > 0.5, 1, 0)


def again_kernel(alphas, weights, p0, q0, grad, turned, rows):
    value = p0[...] - alphas[0] * q0[...]
    step = grad[...] - alphas[0] * turned[...]
    rows[...] = in_lanes([folded(step * step), folded(tile_cols(weights) * value * value)], rows.shape)


def ratio_kernel(alphas, rows, out):
    norm1, curve1 = totals(rows, 2)
    out[0] = alphas[0]
    out[1] = scalar(norm1 / curve1)


def smooth_kernel(ends, alphas, volume, grad, turned, first0, last0, first, last, residual, p0, q0, smoothed, left_over):
    alpha0, alpha1 = alphas[0], alphas[1]
    rest = residual[...] - alpha0 * p0[...] - alpha1 * (p0[...] - alpha0 * q0[...])
    for t in range(rest.shape[0]):
        left_over[:, 128 * t : 128 * t + 128] = rest[t]

    def stepped(x, g, h):
        return x - alpha0 * g - alpha1 * (g - alpha0 * h)

    row = lax.broadcasted_iota(jnp.int32, (48, 128), 0)
    open_link = ~(((row == 7) & (ends[0] == 1)) | ((row == 39) & (ends[1] == 1)))
    link = jnp.where(open_link, F32(1.0), F32(0.0))
    for p in range(grad.shape[0]):
        cols = slice(128 * p, 128 * p + 128)
        last_h, first_h = last[p // 2], first[p // 2]
        if p % 2:
            last_h, first_h = pltpu.roll(last_h, 3, 0), pltpu.roll(first_h, 5, 0)
        ext = jnp.concatenate(
            [
                stepped(last0[p], pltpu.roll(last0[p], 3, 0), last_h),
                stepped(volume[:, cols], grad[p], turned[p]),
                stepped(first0[p], pltpu.roll(first0[p], 5, 0), first_h),
            ],
            axis=0,
        )
        for _ in range(PASSES):
            clipped = jnp.clip(pltpu.roll(ext, 47, 0) - ext, -huber_width, huber_width) * link
            ext = ext + smooth_rate * (clipped - pltpu.roll(clipped, 1, 0))
        smoothed[:, cols] = ext[8:40]


def shift(value, axis, by):
    n = lax.axis_size(axis)
    return lax.ppermute(value, axis, [(i, (i + by) % n) for i in range(n)])


RAY = (8, 32, 128)


def summed_by_owner(mine, theirs):
    got = shift(theirs, "tile_1", 1)
    kept, s1, s2, s3 = call(add_kernel, [RAY] * 4, [mine, got])
    return kept, shift(s1, "tile_0", 1), shift(s2, "tile_0", 2), shift(s3, "tile_0", 3)


def to_everyone(own):
    column = [own] + [shift(own, "tile_0", -r) for r in (1, 2, 3)]
    return column + [shift(block, "tile_1", 1) for block in column]


def over_all(rows):
    return lax.all_to_all(rows, TILE + SLAB, 0, 0, tiled=True)


def shards(volume, measured, weights, footprints, foot_pixel, foot_strip):
    me = jnp.stack([lax.axis_index("tile_0"), lax.axis_index("tile_1")])
    spots = [foot_pixel, foot_strip, me]
    slabs = lax.axis_size(SLAB)
    place_in = lax.axis_index(SLAB)
    ends = jnp.stack([place_in == 0, place_in == slabs - 1]).astype(jnp.int32)
    up = [(i, (i + 1) % slabs) for i in range(slabs)]
    down = [(j, i) for i, j in up]

    field, tile = (32, 32, 128), (1, 8, 128)
    scratch = [pltpu.VMEM(field, BF16), pltpu.VMEM(field, BF16), pltpu.VMEM((64, 32, 128), F32)]
    in_place = [pltpu.with_memory_space_constraint(x, pltpu.HBM) for x in (foot_pixel, foot_strip, footprints, volume)]
    streams = [
        pltpu.VMEM(footprints.shape, F32),
        pltpu.VMEM(volume.shape, F32),
        *scratch,
        pltpu.SMEM(foot_pixel.shape, jnp.int32),
        pltpu.SMEM(foot_strip.shape, jnp.int32),
        pltpu.SemaphoreType.DMA((3,)),
        pltpu.SemaphoreType.DMA((CHUNKS,)),
    ]
    split = jax.ShapeDtypeStruct((64, 128, 256), BF16)
    half, edge = (4,) + RAY, (32, 8, 128)
    mine, theirs, first0, last0, plain, turned = call(
        first_kernel,
        [half, half, edge, edge, split, split],
        [*in_place[:2], me, *in_place[2:]],
        streams,
        3,
        any_at=(0, 1, 3, 4),
        limit=16,
    )
    parts = summed_by_owner(mine, theirs)
    residual, sent = call(start_kernel, [RAY, RAY], [*parts, measured, weights])

    mine, theirs, grad, norm0, first0, last0 = call(
        second_kernel,
        [half, half, field, tile, edge, edge],
        [*spots, plain, turned, *to_everyone(sent), first0, last0],
        scratch,
        3,
    )
    parts = summed_by_owner(mine, theirs)
    first0, last0 = lax.ppermute(first0, SLAB, down), lax.ppermute(last0, SLAB, up)
    sent = call(resend_kernel, [RAY], [*parts, weights])[0]
    late = (*parts, sent)
    pieces = to_everyone(sent)
    pieces, first0, last0 = lax.optimization_barrier((pieces, first0, last0))

    mine, theirs, back, crossed, first, last = call(
        third_kernel,
        [half, half, field, (2, 8, 128), (16, 8, 128), (16, 8, 128)],
        [*spots, plain, turned, *pieces, grad],
        scratch,
        3,
    )
    p0, curve0, spare = call(middle_kernel, [RAY, tile, field], [*late, back])
    parts = summed_by_owner(mine, theirs)
    first, last = lax.ppermute(first, SLAB, down), lax.ppermute(last, SLAB, up)
    everyone = slabs * lax.axis_size(TILE)
    q0, rows = call(
        end_kernel, [RAY, (everyone, 128)], [*parts, weights, p0, norm0, curve0, crossed]
    )
    rows, ends = lax.optimization_barrier((rows, ends))
    rows = over_all(rows)
    alphas, again = pl.pallas_call(
        judge_kernel,
        out_shape=[jax.ShapeDtypeStruct((2,), F32), jax.ShapeDtypeStruct((1,), jnp.int32)],
        in_specs=[VM],
        out_specs=[SM, SM],
        compiler_params=pltpu.CompilerParams(vmem_limit_bytes=8 << 20),
    )(rows)

    def summed_again(alphas):
        rows = call(again_kernel, [(everyone, 128)], [alphas, weights, p0, q0, grad, spare], (), 1)[0]
        return pl.pallas_call(
            ratio_kernel,
            out_shape=jax.ShapeDtypeStruct((2,), F32),
            in_specs=[SM, VM],
            out_specs=SM,
            compiler_params=pltpu.CompilerParams(vmem_limit_bytes=8 << 20),
        )(alphas, over_all(rows))

    alphas = lax.cond(again[0] == 1, summed_again, lambda known: known, alphas)
    return call(
        smooth_kernel,
        [volume.shape, measured.shape],
        [ends, alphas, volume, grad, back, first0, last0, first, last, residual, p0, q0],
        (),
        2,
    )


def solution(mesh):
    finer = Mesh(mesh.devices.reshape(4, 2, 4, 4), ("tile_0", "tile_1", "slab_0", "slab_1"))
    return jax.shard_map(
        lambda *args: tuple(shards(*args)),
        mesh=finer,
        in_specs=(
            P(SLAB, TILE),
            P(SLAB, TILE),
            P(SLAB, TILE),
            P(TILE, None, None),
            P(TILE),
            P(TILE),
        ),
        out_specs=(P(SLAB, TILE), P(SLAB, TILE)),
        check_vma=False,
    )
```

profile of v0, /device:TPU:1, one launch (start us, length us, event | category | flops | bytes accessed | tf_op | source)
XLA Modules:
  0.0 105.4 jit_solution(9478120199989386626)
XLA Ops:
  0.8 5.7 %shard_map.77 = (f32[4,8,32,128]{3,2,1,0:T(8,128)S(1)}, f32[4,8,32,128]{3,2,1,0:T(8,128)S(1)}, f32[32,8,128]{2,1,0:T(8,128)S(1)}, f32[32,8,128]{2,1,0:T(8,128)S(...) custom-call(s32[256]{0:T(256)} %pixels.3, s32[256]{0:T(256)} %strips.3, s32[2]{0:T(128)S(1)} %pad_add_fusion.me, ...), custom_call_target="tpu_custom_call" | custom-call | flops 1000000 | bytes 1048576 | tf_op jit(solution)/shard_map/pallas_call | solution.py:30
  6.5 1.5 %collective-permute-start = (f32[4,8,32,128]{3,2,1,0:T(8,128)S(1)}, f32[4,8,32,128]{3,2,1,0:T(8,128)S(1)}, u32[]{:S(2)}, u32[]{:S(2)}) collective-permute-start(f32[4,8,32,128]{3,2,1,0:T(8,128)S(1)} %get-tuple-element.78), channel_id=1, source_target_pairs={{0,16},{16,0},{1,17},{17,1},{2,18},{18,2},{3,19},{19,3},{4,20},{20... | collective-permute-start | bytes 1572872 | tf_op jit(solution)/shard_map/ppermute | solution.py:316
  8.0 1.5 %collective-permute-done.got = f32[4,8,32,128]{3,2,1,0:T(8,128)S(1)} collective-permute-done((f32[4,8,32,128]{3,2,1,0:T(8,128)S(1)}, f32[4,8,32,128]{3,2,1,0:T(8,128)S(1)}, u32[]{:S(2)}, u32[]{:S(2)}) %collective-permute-start) | collective-permute-done | bytes 524320 | tf_op jit(solution)/shard_map/ppermute | solution.py:316
  9.6 1.5 %collective-permute-start.1 = (f32[8,32,128]{2,1,0:T(8,128)S(1)}, f32[8,32,128]{2,1,0:T(8,128)S(1)}, u32[]{:S(2)}, u32[]{:S(2)}) collective-permute-start(f32[8,32,128]{2,1,0:T(8,128)S(1)} %get-tuple-element.80), channel_id=1, source_target_pairs={{0,32},{32,64},{64,96},{96,0},{1,33},{33,65},{65,97},{97,1},{2,34}... | collective-permute-start | bytes 393224 | tf_op jit(solution)/shard_map/ppermute | solution.py:316
  11.0 2.6 %collective-permute-start.2 = (f32[8,32,128]{2,1,0:T(8,128)S(1)}, f32[8,32,128]{2,1,0:T(8,128)S(1)}, u32[]{:S(2)}, u32[]{:S(2)}) collective-permute-start(f32[8,32,128]{2,1,0:T(8,128)S(1)} %get-tuple-element.81), channel_id=1, source_target_pairs={{0,64},{32,96},{64,0},{96,32},{1,65},{33,97},{65,1},{97,33},{2,66}... | collective-permute-start | bytes 393224 | tf_op jit(solution)/shard_map/ppermute | solution.py:316
  15.9 3.8 %collective-permute-done.2.b = f32[8,32,128]{2,1,0:T(8,128)S(1)} collective-permute-done((f32[8,32,128]{2,1,0:T(8,128)S(1)}, f32[8,32,128]{2,1,0:T(8,128)S(1)}, u32[]{:S(2)}, u32[]{:S(2)}) %collective-permute-start.2) | collective-permute-done | bytes 131104 | tf_op jit(solution)/shard_map/ppermute | solution.py:316
  20.8 2.3 %collective-permute-start.5 = (f32[8,32,128]{2,1,0:T(8,128)S(1)}, f32[8,32,128]{2,1,0:T(8,128)S(1)}, u32[]{:S(2)}, u32[]{:S(2)}) collective-permute-start(f32[8,32,128]{2,1,0:T(8,128)S(1)} %get-tuple-element.83.refs_0_), channel_id=1, source_target_pairs={{0,64},{32,96},{64,0},{96,32},{1,65},{33,97},{65,1},{97,33},{2,66}... | collective-permute-start | bytes 393224 | tf_op jit(solution)/shard_map/ppermute | solution.py:316
  23.9 2.3 %collective-permute-start.7 = (f32[8,32,128]{2,1,0:T(8,128)S(1)}, f32[8,32,128]{2,1,0:T(8,128)S(1)}, u32[]{:S(2)}, u32[]{:S(2)}) collective-permute-start(f32[8,32,128]{2,1,0:T(8,128)S(1)} %get-tuple-element.83.refs_0_), channel_id=1, source_target_pairs={{0,16},{16,0},{1,17},{17,1},{2,18},{18,2},{3,19},{19,3},{4,20},{20... | collective-permute-start | bytes 393224 | tf_op jit(solution)/shard_map/ppermute | solution.py:316
  26.2 2.2 %collective-permute-start.10 = (f32[8,32,128]{2,1,0:T(8,128)S(1)}, f32[8,32,128]{2,1,0:T(8,128)S(1)}, u32[]{:S(2)}, u32[]{:S(2)}) collective-permute-start(f32[8,32,128]{2,1,0:T(8,128)S(1)} %collective-permute-done.6.refs_3_), channel_id=1, source_target_pairs={{0,16},{16,0},{1,17},{17,1},{2,18},{18,2},{3,19},{19,3},{4,20},{20... | collective-permute-start | bytes 393224 | tf_op jit(solution)/shard_map/ppermute | solution.py:316
  28.4 1.9 %collective-permute-start.9 = (f32[8,32,128]{2,1,0:T(8,128)S(1)}, f32[8,32,128]{2,1,0:T(8,128)S(1)}, u32[]{:S(2)}, u32[]{:S(2)}) collective-permute-start(f32[8,32,128]{2,1,0:T(8,128)S(1)} %collective-permute-done.5.refs_2_), channel_id=1, source_target_pairs={{0,16},{16,0},{1,17},{17,1},{2,18},{18,2},{3,19},{19,3},{4,20},{20... | collective-permute-start | bytes 393224 | tf_op jit(solution)/shard_map/ppermute | solution.py:316
  31.7 5.8 %shard_map.80 = (f32[4,8,32,128]{3,2,1,0:T(8,128)S(1)}, f32[4,8,32,128]{3,2,1,0:T(8,128)S(1)}, f32[32,32,128]{2,1,0:T(8,128)S(1)}, f32[1,8,128]{2,1,0:T(8,128)S(...) custom-call(s32[256]{0:T(256)S(1)} %copy-done.2, s32[256]{0:T(256)S(1)} %copy-done.3, s32[2]{0:T(128)S(1)} %pad_add_fusion.me, ...), custom_call_target="tpu_custom_call" | custom-call | flops 1000000 | bytes 1048576 | tf_op jit(solution)/shard_map/pallas_call | solution.py:30
  37.7 1.7 %collective-permute-done.11.got = f32[4,8,32,128]{3,2,1,0:T(8,128)S(1)} collective-permute-done((f32[4,8,32,128]{3,2,1,0:T(8,128)S(1)}, f32[4,8,32,128]{3,2,1,0:T(8,128)S(1)}, u32[]{:S(2)}, u32[]{:S(2)}) %collective-permute-start.11) | collective-permute-done | bytes 524320 | tf_op jit(solution)/shard_map/ppermute | solution.py:316
  40.7 2.1 %collective-permute-start.13 = (f32[8,32,128]{2,1,0:T(8,128)S(1)}, f32[8,32,128]{2,1,0:T(8,128)S(1)}, u32[]{:S(2)}, u32[]{:S(2)}) collective-permute-start(f32[8,32,128]{2,1,0:T(8,128)S(1)} %get-tuple-element.90), channel_id=1, source_target_pairs={{0,64},{32,96},{64,0},{96,32},{1,65},{33,97},{65,1},{97,33},{2,66}... | collective-permute-start | bytes 393224 | tf_op jit(solution)/shard_map/ppermute | solution.py:316
  43.4 5.9 %collective-permute-start.22 = (f32[32,8,128]{2,1,0:T(8,128)S(1)}, f32[32,8,128]{2,1,0:T(8,128)S(1)}, u32[]{:S(2)}, u32[]{:S(2)}) collective-permute-start(f32[32,8,128]{2,1,0:T(8,128)S(1)} %get-tuple-element.92), channel_id=1, source_target_pairs={{1,0},{2,1},{3,2},{4,3},{5,4},{6,5},{7,6},{8,7},{9,8},{10,9},{11,1... | collective-permute-start | bytes 393224 | tf_op jit(solution)/shard_map/ppermute | solution.py:380
  49.4 1.6 %collective-permute-start.17 = (f32[8,32,128]{2,1,0:T(8,128)S(1)}, f32[8,32,128]{2,1,0:T(8,128)S(1)}, u32[]{:S(2)}, u32[]{:S(2)}) collective-permute-start(f32[8,32,128]{2,1,0:T(8,128)S(1)} %shard_map.82.refs_0_.sent), channel_id=1, source_target_pairs={{0,32},{32,64},{64,96},{96,0},{1,33},{33,65},{65,97},{97,1},{2,34}... | collective-permute-start | bytes 393224 | tf_op jit(solution)/shard_map/ppermute | solution.py:316
  51.0 2.4 %collective-permute-start.16 = (f32[8,32,128]{2,1,0:T(8,128)S(1)}, f32[8,32,128]{2,1,0:T(8,128)S(1)}, u32[]{:S(2)}, u32[]{:S(2)}) collective-permute-start(f32[8,32,128]{2,1,0:T(8,128)S(1)} %shard_map.82.refs_0_.sent), channel_id=1, source_target_pairs={{0,64},{32,96},{64,0},{96,32},{1,65},{33,97},{65,1},{97,33},{2,66}... | collective-permute-start | bytes 393224 | tf_op jit(solution)/shard_map/ppermute | solution.py:316
  53.5 1.2 %collective-permute-start.23 = (f32[32,8,128]{2,1,0:T(8,128)S(1)}, f32[32,8,128]{2,1,0:T(8,128)S(1)}, u32[]{:S(2)}, u32[]{:S(2)}) collective-permute-start(f32[32,8,128]{2,1,0:T(8,128)S(1)} %get-tuple-element.93), channel_id=1, source_target_pairs={{0,1},{1,2},{2,3},{3,4},{4,5},{5,6},{6,7},{7,8},{8,9},{9,10},{10,1... | collective-permute-start | bytes 393224 | tf_op jit(solution)/shard_map/ppermute | solution.py:380
  54.7 1.8 %collective-permute-start.18 = (f32[8,32,128]{2,1,0:T(8,128)S(1)}, f32[8,32,128]{2,1,0:T(8,128)S(1)}, u32[]{:S(2)}, u32[]{:S(2)}) collective-permute-start(f32[8,32,128]{2,1,0:T(8,128)S(1)} %shard_map.82.refs_0_.sent), channel_id=1, source_target_pairs={{0,16},{16,0},{1,17},{17,1},{2,18},{18,2},{3,19},{19,3},{4,20},{20... | collective-permute-start | bytes 393224 | tf_op jit(solution)/shard_map/ppermute | solution.py:316
  56.5 1.2 %collective-permute-start.21 = (f32[8,32,128]{2,1,0:T(8,128)S(1)}, f32[8,32,128]{2,1,0:T(8,128)S(1)}, u32[]{:S(2)}, u32[]{:S(2)}) collective-permute-start(f32[8,32,128]{2,1,0:T(8,128)S(1)} %collective-permute-done.17.refs_3_), channel_id=1, source_target_pairs={{0,16},{16,0},{1,17},{17,1},{2,18},{18,2},{3,19},{19,3},{4,20},{20... | collective-permute-start | bytes 393224 | tf_op jit(solution)/shard_map/ppermute | solution.py:316
  57.7 1.6 %collective-permute-done.16.refs_2_ = f32[8,32,128]{2,1,0:T(8,128)S(1)} collective-permute-done((f32[8,32,128]{2,1,0:T(8,128)S(1)}, f32[8,32,128]{2,1,0:T(8,128)S(1)}, u32[]{:S(2)}, u32[]{:S(2)}) %collective-permute-start.16) | collective-permute-done | bytes 131104 | tf_op jit(solution)/shard_map/ppermute | solution.py:316
  59.3 1.4 %collective-permute-start.20 = (f32[8,32,128]{2,1,0:T(8,128)S(1)}, f32[8,32,128]{2,1,0:T(8,128)S(1)}, u32[]{:S(2)}, u32[]{:S(2)}) collective-permute-start(f32[8,32,128]{2,1,0:T(8,128)S(1)} %collective-permute-done.16.refs_2_), channel_id=1, source_target_pairs={{0,16},{16,0},{1,17},{17,1},{2,18},{18,2},{3,19},{19,3},{4,20},{20... | collective-permute-start | bytes 393224 | tf_op jit(solution)/shard_map/ppermute | solution.py:316
  62.0 5.8 %shard_map.83 = (f32[4,8,32,128]{3,2,1,0:T(8,128)S(1)}, f32[4,8,32,128]{3,2,1,0:T(8,128)S(1)}, f32[32,32,128]{2,1,0:T(8,128)S(1)}, f32[2,8,128]{2,1,0:T(8,128)S(...) custom-call(s32[256]{0:T(256)S(1)} %copy-done.2, s32[256]{0:T(256)S(1)} %copy-done.3, s32[2]{0:T(128)S(1)} %pad_add_fusion.me, ...), custom_call_target="tpu_custom_call" | custom-call | flops 1000000 | bytes 1048576 | tf_op jit(solution)/shard_map/pallas_call | solution.py:30
  67.8 2.2 %collective-permute-start.24 = (f32[4,8,32,128]{3,2,1,0:T(8,128)S(1)}, f32[4,8,32,128]{3,2,1,0:T(8,128)S(1)}, u32[]{:S(2)}, u32[]{:S(2)}) collective-permute-start(f32[4,8,32,128]{3,2,1,0:T(8,128)S(1)} %get-tuple-element.104), channel_id=1, source_target_pairs={{0,16},{16,0},{1,17},{17,1},{2,18},{18,2},{3,19},{19,3},{4,20},{20... | collective-permute-start | bytes 1572872 | tf_op jit(solution)/shard_map/ppermute | solution.py:316
  70.1 1.5 %collective-permute-done.24.got = f32[4,8,32,128]{3,2,1,0:T(8,128)S(1)} collective-permute-done((f32[4,8,32,128]{3,2,1,0:T(8,128)S(1)}, f32[4,8,32,128]{3,2,1,0:T(8,128)S(1)}, u32[]{:S(2)}, u32[]{:S(2)}) %collective-permute-start.24) | collective-permute-done | bytes 524320 | tf_op jit(solution)/shard_map/ppermute | solution.py:316
  71.7 1.3 %collective-permute-start.25 = (f32[8,32,128]{2,1,0:T(8,128)S(1)}, f32[8,32,128]{2,1,0:T(8,128)S(1)}, u32[]{:S(2)}, u32[]{:S(2)}) collective-permute-start(f32[8,32,128]{2,1,0:T(8,128)S(1)} %get-tuple-element.106), channel_id=1, source_target_pairs={{0,32},{32,64},{64,96},{96,0},{1,33},{33,65},{65,97},{97,1},{2,34}... | collective-permute-start | bytes 393224 | tf_op jit(solution)/shard_map/ppermute | solution.py:316
  73.5 2.0 %collective-permute-start.27 = (f32[8,32,128]{2,1,0:T(8,128)S(1)}, f32[8,32,128]{2,1,0:T(8,128)S(1)}, u32[]{:S(2)}, u32[]{:S(2)}) collective-permute-start(f32[8,32,128]{2,1,0:T(8,128)S(1)} %get-tuple-element.108), channel_id=1, source_target_pairs={{0,96},{32,0},{64,32},{96,64},{1,97},{33,1},{65,33},{97,65},{2,98}... | collective-permute-start | bytes 393224 | tf_op jit(solution)/shard_map/ppermute | solution.py:316
  76.4 1.5 %collective-permute-done.25.a = f32[8,32,128]{2,1,0:T(8,128)S(1)} collective-permute-done((f32[8,32,128]{2,1,0:T(8,128)S(1)}, f32[8,32,128]{2,1,0:T(8,128)S(1)}, u32[]{:S(2)}, u32[]{:S(2)}) %collective-permute-start.25) | collective-permute-done | bytes 131104 | tf_op jit(solution)/shard_map/ppermute | solution.py:316
  77.9 1.6 %collective-permute-done.26.b = f32[8,32,128]{2,1,0:T(8,128)S(1)} collective-permute-done((f32[8,32,128]{2,1,0:T(8,128)S(1)}, f32[8,32,128]{2,1,0:T(8,128)S(1)}, u32[]{:S(2)}, u32[]{:S(2)}) %collective-permute-start.26) | collective-permute-done | bytes 131104 | tf_op jit(solution)/shard_map/ppermute | solution.py:316
  81.6 9.1 %all-to-all-start.1 = ((f32[128,1,128]{2,1,0:T(1,128)}), f32[128,1,128]{2,1,0:T(1,128)S(1)}, u32[]{:S(2)}, u32[]{:S(2)}) async-start(f32[128,1,128]{2,1,0:T(1,128)} %bitcast.9), calls=%async_computation.1 | async-start | bytes 131072 | tf_op jit(solution)/shard_map/all_to_all | solution.py:334
  90.8 5.5 %collective-permute-start.28 = (f32[16,8,128]{2,1,0:T(8,128)S(1)}, f32[16,8,128]{2,1,0:T(8,128)S(1)}, u32[]{:S(2)}, u32[]{:S(2)}) collective-permute-start(f32[16,8,128]{2,1,0:T(8,128)S(1)} %get-tuple-element.123), channel_id=1, source_target_pairs={{1,0},{2,1},{3,2},{4,3},{5,4},{6,5},{7,6},{8,7},{9,8},{10,9},{11,1... | collective-permute-start | bytes 196616 | tf_op jit(solution)/shard_map/ppermute | solution.py:395
  96.2 4.3 %all-to-all-done.1 = f32[128,1,128]{2,1,0:T(1,128)S(1)} async-done(((f32[128,1,128]{2,1,0:T(1,128)}), f32[128,1,128]{2,1,0:T(1,128)S(1)}, u32[]{:S(2)}, u32[]{:S(2)}) %all-to-all-start.1) | async-done | bytes 65568 | tf_op jit(solution)/shard_map/all_to_all | solution.py:334
  102.7 2.7 %shard_map.88 = (f32[32,4096]{1,0:T(8,128)}, f32[32,1024]{1,0:T(8,128)}) custom-call(s32[2]{0:T(128)S(1)} %add_convert_fusion.ends, f32[2]{0:T(128)S(1)} %get-tuple-element.126.alphas, f32[32,4096]{1,0:T(8,128)S(1)} %copy-done, f32[32,32,128]{2,1,0:T(8,128)} %copy-done.4, f32[32,32,128]{2,1,0:T(8,128)S(1)} %get-tuple-element.109.back.turned, ...), custom_call_target="tpu_custom_call" | custom-call | flops 1000000 | bytes 1048576 | tf_op jit(solution)/shard_map/pallas_call | solution.py:30
  (57 shorter events, 14.2 us)
Async XLA Ops:
  6.5 3.0 %collective-permute-start = (f32[4,8,32,128]{3,2,1,0:T(8,128)S(1)}, f32[4,8,32,128]{3,2,1,0:T(8,128)S(1)}, u32[]{:S(2)}, u32[]{:S(2)}) collective-permute-start(f32[4,8,32,128]{3,2,1,0:T(8,128)S(1)} %get-tuple-element.78), channel_id=1, source_target_pairs={{0,16},{16,0},{1,17},{17,1},{2,18},{18,2},{3,19},{19,3},{4,20},{20... | collective-permute-start | bytes 1572872 | tf_op jit(solution)/shard_map/ppermute | solution.py:316
  9.6 6.3 %collective-permute-start.1 = (f32[8,32,128]{2,1,0:T(8,128)S(1)}, f32[8,32,128]{2,1,0:T(8,128)S(1)}, u32[]{:S(2)}, u32[]{:S(2)}) collective-permute-start(f32[8,32,128]{2,1,0:T(8,128)S(1)} %get-tuple-element.80), channel_id=1, source_target_pairs={{0,32},{32,64},{64,96},{96,0},{1,33},{33,65},{65,97},{97,1},{2,34}... | collective-permute-start | bytes 393224 | tf_op jit(solution)/shard_map/ppermute | solution.py:316
  11.0 8.7 %collective-permute-start.2 = (f32[8,32,128]{2,1,0:T(8,128)S(1)}, f32[8,32,128]{2,1,0:T(8,128)S(1)}, u32[]{:S(2)}, u32[]{:S(2)}) collective-permute-start(f32[8,32,128]{2,1,0:T(8,128)S(1)} %get-tuple-element.81), channel_id=1, source_target_pairs={{0,64},{32,96},{64,0},{96,32},{1,65},{33,97},{65,1},{97,33},{2,66}... | collective-permute-start | bytes 393224 | tf_op jit(solution)/shard_map/ppermute | solution.py:316
  13.6 6.0 %collective-permute-start.3 = (f32[8,32,128]{2,1,0:T(8,128)S(1)}, f32[8,32,128]{2,1,0:T(8,128)S(1)}, u32[]{:S(2)}, u32[]{:S(2)}) collective-permute-start(f32[8,32,128]{2,1,0:T(8,128)S(1)} %get-tuple-element.82), channel_id=1, source_target_pairs={{0,96},{32,0},{64,32},{96,64},{1,97},{33,1},{65,33},{97,65},{2,98}... | collective-permute-start | bytes 393224 | tf_op jit(solution)/shard_map/ppermute | solution.py:316
  19.7 6.5 %collective-permute-start.6 = (f32[8,32,128]{2,1,0:T(8,128)S(1)}, f32[8,32,128]{2,1,0:T(8,128)S(1)}, u32[]{:S(2)}, u32[]{:S(2)}) collective-permute-start(f32[8,32,128]{2,1,0:T(8,128)S(1)} %get-tuple-element.83.refs_0_), channel_id=1, source_target_pairs={{0,32},{32,64},{64,96},{96,0},{1,33},{33,65},{65,97},{97,1},{2,34}... | collective-permute-start | bytes 393224 | tf_op jit(solution)/shard_map/ppermute | solution.py:316
  20.8 7.6 %collective-permute-start.5 = (f32[8,32,128]{2,1,0:T(8,128)S(1)}, f32[8,32,128]{2,1,0:T(8,128)S(1)}, u32[]{:S(2)}, u32[]{:S(2)}) collective-permute-start(f32[8,32,128]{2,1,0:T(8,128)S(1)} %get-tuple-element.83.refs_0_), channel_id=1, source_target_pairs={{0,64},{32,96},{64,0},{96,32},{1,65},{33,97},{65,1},{97,33},{2,66}... | collective-permute-start | bytes 393224 | tf_op jit(solution)/shard_map/ppermute | solution.py:316
  23.0 7.3 %collective-permute-start.4 = (f32[8,32,128]{2,1,0:T(8,128)S(1)}, f32[8,32,128]{2,1,0:T(8,128)S(1)}, u32[]{:S(2)}, u32[]{:S(2)}) collective-permute-start(f32[8,32,128]{2,1,0:T(8,128)S(1)} %get-tuple-element.83.refs_0_), channel_id=1, source_target_pairs={{0,96},{32,0},{64,32},{96,64},{1,97},{33,1},{65,33},{97,65},{2,98}... | collective-permute-start | bytes 393224 | tf_op jit(solution)/shard_map/ppermute | solution.py:316
  23.9 6.4 %collective-permute-start.7 = (f32[8,32,128]{2,1,0:T(8,128)S(1)}, f32[8,32,128]{2,1,0:T(8,128)S(1)}, u32[]{:S(2)}, u32[]{:S(2)}) collective-permute-start(f32[8,32,128]{2,1,0:T(8,128)S(1)} %get-tuple-element.83.refs_0_), channel_id=1, source_target_pairs={{0,16},{16,0},{1,17},{17,1},{2,18},{18,2},{3,19},{19,3},{4,20},{20... | collective-permute-start | bytes 393224 | tf_op jit(solution)/shard_map/ppermute | solution.py:316
  26.2 4.1 %collective-permute-start.10 = (f32[8,32,128]{2,1,0:T(8,128)S(1)}, f32[8,32,128]{2,1,0:T(8,128)S(1)}, u32[]{:S(2)}, u32[]{:S(2)}) collective-permute-start(f32[8,32,128]{2,1,0:T(8,128)S(1)} %collective-permute-done.6.refs_3_), channel_id=1, source_target_pairs={{0,16},{16,0},{1,17},{17,1},{2,18},{18,2},{3,19},{19,3},{4,20},{20... | collective-permute-start | bytes 393224 | tf_op jit(solution)/shard_map/ppermute | solution.py:316
  28.4 2.9 %collective-permute-start.9 = (f32[8,32,128]{2,1,0:T(8,128)S(1)}, f32[8,32,128]{2,1,0:T(8,128)S(1)}, u32[]{:S(2)}, u32[]{:S(2)}) collective-permute-start(f32[8,32,128]{2,1,0:T(8,128)S(1)} %collective-permute-done.5.refs_2_), channel_id=1, source_target_pairs={{0,16},{16,0},{1,17},{17,1},{2,18},{18,2},{3,19},{19,3},{4,20},{20... | collective-permute-start | bytes 393224 | tf_op jit(solution)/shard_map/ppermute | solution.py:316
  30.3 1.3 %collective-permute-start.8 = (f32[8,32,128]{2,1,0:T(8,128)S(1)}, f32[8,32,128]{2,1,0:T(8,128)S(1)}, u32[]{:S(2)}, u32[]{:S(2)}) collective-permute-start(f32[8,32,128]{2,1,0:T(8,128)S(1)} %collective-permute-done.4.refs_1_), channel_id=1, source_target_pairs={{0,16},{16,0},{1,17},{17,1},{2,18},{18,2},{3,19},{19,3},{4,20},{20... | collective-permute-start | bytes 393224 | tf_op jit(solution)/shard_map/ppermute | solution.py:316
  37.5 2.0 %collective-permute-start.11 = (f32[4,8,32,128]{3,2,1,0:T(8,128)S(1)}, f32[4,8,32,128]{3,2,1,0:T(8,128)S(1)}, u32[]{:S(2)}, u32[]{:S(2)}) collective-permute-start(f32[4,8,32,128]{3,2,1,0:T(8,128)S(1)} %get-tuple-element.87), channel_id=1, source_target_pairs={{0,16},{16,0},{1,17},{17,1},{2,18},{18,2},{3,19},{19,3},{4,20},{20... | collective-permute-start | bytes 1572872 | tf_op jit(solution)/shard_map/ppermute | solution.py:316
  39.5 9.8 %collective-permute-start.12 = (f32[8,32,128]{2,1,0:T(8,128)S(1)}, f32[8,32,128]{2,1,0:T(8,128)S(1)}, u32[]{:S(2)}, u32[]{:S(2)}) collective-permute-start(f32[8,32,128]{2,1,0:T(8,128)S(1)} %get-tuple-element.89), channel_id=1, source_target_pairs={{0,32},{32,64},{64,96},{96,0},{1,33},{33,65},{65,97},{97,1},{2,34}... | collective-permute-start | bytes 393224 | tf_op jit(solution)/shard_map/ppermute | solution.py:316
  40.7 8.6 %collective-permute-start.13 = (f32[8,32,128]{2,1,0:T(8,128)S(1)}, f32[8,32,128]{2,1,0:T(8,128)S(1)}, u32[]{:S(2)}, u32[]{:S(2)}) collective-permute-start(f32[8,32,128]{2,1,0:T(8,128)S(1)} %get-tuple-element.90), channel_id=1, source_target_pairs={{0,64},{32,96},{64,0},{96,32},{1,65},{33,97},{65,1},{97,33},{2,66}... | collective-permute-start | bytes 393224 | tf_op jit(solution)/shard_map/ppermute | solution.py:316
  42.8 6.5 %collective-permute-start.14 = (f32[8,32,128]{2,1,0:T(8,128)S(1)}, f32[8,32,128]{2,1,0:T(8,128)S(1)}, u32[]{:S(2)}, u32[]{:S(2)}) collective-permute-start(f32[8,32,128]{2,1,0:T(8,128)S(1)} %get-tuple-element.91), channel_id=1, source_target_pairs={{0,96},{32,0},{64,32},{96,64},{1,97},{33,1},{65,33},{97,65},{2,98}... | collective-permute-start | bytes 393224 | tf_op jit(solution)/shard_map/ppermute | solution.py:316
  43.4 11.3 %collective-permute-start.22 = (f32[32,8,128]{2,1,0:T(8,128)S(1)}, f32[32,8,128]{2,1,0:T(8,128)S(1)}, u32[]{:S(2)}, u32[]{:S(2)}) collective-permute-start(f32[32,8,128]{2,1,0:T(8,128)S(1)} %get-tuple-element.92), channel_id=1, source_target_pairs={{1,0},{2,1},{3,2},{4,3},{5,4},{6,5},{7,6},{8,7},{9,8},{10,9},{11,1... | collective-permute-start | bytes 393224 | tf_op jit(solution)/shard_map/ppermute | solution.py:380
  49.4 7.1 %collective-permute-start.17 = (f32[8,32,128]{2,1,0:T(8,128)S(1)}, f32[8,32,128]{2,1,0:T(8,128)S(1)}, u32[]{:S(2)}, u32[]{:S(2)}) collective-permute-start(f32[8,32,128]{2,1,0:T(8,128)S(1)} %shard_map.82.refs_0_.sent), channel_id=1, source_target_pairs={{0,32},{32,64},{64,96},{96,0},{1,33},{33,65},{65,97},{97,1},{2,34}... | collective-permute-start | bytes 393224 | tf_op jit(solution)/shard_map/ppermute | solution.py:316
  51.0 8.3 %collective-permute-start.16 = (f32[8,32,128]{2,1,0:T(8,128)S(1)}, f32[8,32,128]{2,1,0:T(8,128)S(1)}, u32[]{:S(2)}, u32[]{:S(2)}) collective-permute-start(f32[8,32,128]{2,1,0:T(8,128)S(1)} %shard_map.82.refs_0_.sent), channel_id=1, source_target_pairs={{0,64},{32,96},{64,0},{96,32},{1,65},{33,97},{65,1},{97,33},{2,66}... | collective-permute-start | bytes 393224 | tf_op jit(solution)/shard_map/ppermute | solution.py:316
  53.4 7.3 %collective-permute-start.15 = (f32[8,32,128]{2,1,0:T(8,128)S(1)}, f32[8,32,128]{2,1,0:T(8,128)S(1)}, u32[]{:S(2)}, u32[]{:S(2)}) collective-permute-start(f32[8,32,128]{2,1,0:T(8,128)S(1)} %shard_map.82.refs_0_.sent), channel_id=1, source_target_pairs={{0,96},{32,0},{64,32},{96,64},{1,97},{33,1},{65,33},{97,65},{2,98}... | collective-permute-start | bytes 393224 | tf_op jit(solution)/shard_map/ppermute | solution.py:316
  53.5 8.3 %collective-permute-start.23 = (f32[32,8,128]{2,1,0:T(8,128)S(1)}, f32[32,8,128]{2,1,0:T(8,128)S(1)}, u32[]{:S(2)}, u32[]{:S(2)}) collective-permute-start(f32[32,8,128]{2,1,0:T(8,128)S(1)} %get-tuple-element.93), channel_id=1, source_target_pairs={{0,1},{1,2},{2,3},{3,4},{4,5},{5,6},{6,7},{7,8},{8,9},{9,10},{10,1... | collective-permute-start | bytes 393224 | tf_op jit(solution)/shard_map/ppermute | solution.py:380
  54.7 7.1 %collective-permute-start.18 = (f32[8,32,128]{2,1,0:T(8,128)S(1)}, f32[8,32,128]{2,1,0:T(8,128)S(1)}, u32[]{:S(2)}, u32[]{:S(2)}) collective-permute-start(f32[8,32,128]{2,1,0:T(8,128)S(1)} %shard_map.82.refs_0_.sent), channel_id=1, source_target_pairs={{0,16},{16,0},{1,17},{17,1},{2,18},{18,2},{3,19},{19,3},{4,20},{20... | collective-permute-start | bytes 393224 | tf_op jit(solution)/shard_map/ppermute | solution.py:316
  56.5 5.3 %collective-permute-start.21 = (f32[8,32,128]{2,1,0:T(8,128)S(1)}, f32[8,32,128]{2,1,0:T(8,128)S(1)}, u32[]{:S(2)}, u32[]{:S(2)}) collective-permute-start(f32[8,32,128]{2,1,0:T(8,128)S(1)} %collective-permute-done.17.refs_3_), channel_id=1, source_target_pairs={{0,16},{16,0},{1,17},{17,1},{2,18},{18,2},{3,19},{19,3},{4,20},{20... | collective-permute-start | bytes 393224 | tf_op jit(solution)/shard_map/ppermute | solution.py:316
  59.3 2.5 %collective-permute-start.20 = (f32[8,32,128]{2,1,0:T(8,128)S(1)}, f32[8,32,128]{2,1,0:T(8,128)S(1)}, u32[]{:S(2)}, u32[]{:S(2)}) collective-permute-start(f32[8,32,128]{2,1,0:T(8,128)S(1)} %collective-permute-done.16.refs_2_), channel_id=1, source_target_pairs={{0,16},{16,0},{1,17},{17,1},{2,18},{18,2},{3,19},{19,3},{4,20},{20... | collective-permute-start | bytes 393224 | tf_op jit(solution)/shard_map/ppermute | solution.py:316
  60.7 1.3 %collective-permute-start.19 = (f32[8,32,128]{2,1,0:T(8,128)S(1)}, f32[8,32,128]{2,1,0:T(8,128)S(1)}, u32[]{:S(2)}, u32[]{:S(2)}) collective-permute-start(f32[8,32,128]{2,1,0:T(8,128)S(1)} %collective-permute-done.15.refs_1_), channel_id=1, source_target_pairs={{0,16},{16,0},{1,17},{17,1},{2,18},{18,2},{3,19},{19,3},{4,20},{20... | collective-permute-start | bytes 393224 | tf_op jit(solution)/shard_map/ppermute | solution.py:316
  67.8 34.9 %copy-start = (f32[32,4096]{1,0:T(8,128)S(1)}, f32[32,4096]{1,0:T(8,128)}, u32[]{:S(2)}) copy-start(f32[32,4096]{1,0:T(8,128)} %volume.1) | copy-start | bytes 1572868
  67.8 3.8 %collective-permute-start.24 = (f32[4,8,32,128]{3,2,1,0:T(8,128)S(1)}, f32[4,8,32,128]{3,2,1,0:T(8,128)S(1)}, u32[]{:S(2)}, u32[]{:S(2)}) collective-permute-start(f32[4,8,32,128]{3,2,1,0:T(8,128)S(1)} %get-tuple-element.104), channel_id=1, source_target_pairs={{0,16},{16,0},{1,17},{17,1},{2,18},{18,2},{3,19},{19,3},{4,20},{20... | collective-permute-start | bytes 1572872 | tf_op jit(solution)/shard_map/ppermute | solution.py:316
  71.7 6.3 %collective-permute-start.25 = (f32[8,32,128]{2,1,0:T(8,128)S(1)}, f32[8,32,128]{2,1,0:T(8,128)S(1)}, u32[]{:S(2)}, u32[]{:S(2)}) collective-permute-start(f32[8,32,128]{2,1,0:T(8,128)S(1)} %get-tuple-element.106), channel_id=1, source_target_pairs={{0,32},{32,64},{64,96},{96,0},{1,33},{33,65},{65,97},{97,1},{2,34}... | collective-permute-start | bytes 393224 | tf_op jit(solution)/shard_map/ppermute | solution.py:316
  73.0 6.6 %collective-permute-start.26 = (f32[8,32,128]{2,1,0:T(8,128)S(1)}, f32[8,32,128]{2,1,0:T(8,128)S(1)}, u32[]{:S(2)}, u32[]{:S(2)}) collective-permute-start(f32[8,32,128]{2,1,0:T(8,128)S(1)} %get-tuple-element.107), channel_id=1, source_target_pairs={{0,64},{32,96},{64,0},{96,32},{1,65},{33,97},{65,1},{97,33},{2,66}... | collective-permute-start | bytes 393224 | tf_op jit(solution)/shard_map/ppermute | solution.py:316
  73.5 7.2 %collective-permute-start.27 = (f32[8,32,128]{2,1,0:T(8,128)S(1)}, f32[8,32,128]{2,1,0:T(8,128)S(1)}, u32[]{:S(2)}, u32[]{:S(2)}) collective-permute-start(f32[8,32,128]{2,1,0:T(8,128)S(1)} %get-tuple-element.108), channel_id=1, source_target_pairs={{0,96},{32,0},{64,32},{96,64},{1,97},{33,1},{65,33},{97,65},{2,98}... | collective-permute-start | bytes 393224 | tf_op jit(solution)/shard_map/ppermute | solution.py:316
  81.6 18.9 %all-to-all-start.1 = ((f32[128,1,128]{2,1,0:T(1,128)}), f32[128,1,128]{2,1,0:T(1,128)S(1)}, u32[]{:S(2)}, u32[]{:S(2)}) async-start(f32[128,1,128]{2,1,0:T(1,128)} %bitcast.9), calls=%async_computation.1 | async-start | bytes 131072 | tf_op jit(solution)/shard_map/all_to_all | solution.py:334
  90.8 11.2 %collective-permute-start.28 = (f32[16,8,128]{2,1,0:T(8,128)S(1)}, f32[16,8,128]{2,1,0:T(8,128)S(1)}, u32[]{:S(2)}, u32[]{:S(2)}) collective-permute-start(f32[16,8,128]{2,1,0:T(8,128)S(1)} %get-tuple-element.123), channel_id=1, source_target_pairs={{1,0},{2,1},{3,2},{4,3},{5,4},{6,5},{7,6},{8,7},{9,8},{10,9},{11,1... | collective-permute-start | bytes 196616 | tf_op jit(solution)/shard_map/ppermute | solution.py:395
  96.2 6.4 %collective-permute-start.29 = (f32[16,8,128]{2,1,0:T(8,128)S(1)}, f32[16,8,128]{2,1,0:T(8,128)S(1)}, u32[]{:S(2)}, u32[]{:S(2)}) collective-permute-start(f32[16,8,128]{2,1,0:T(8,128)S(1)} %get-tuple-element.124), channel_id=1, source_target_pairs={{0,1},{1,2},{2,3},{3,4},{4,5},{5,6},{6,7},{7,8},{8,9},{9,10},{10,1... | collective-permute-start | bytes 196616 | tf_op jit(solution)/shard_map/ppermute | solution.py:395
  (5 other events, 130.4 us)
where the time goes:
time: 106 us; the launch traced here: 105 us
  starting transfers between devices  57.7 us (54%)
  waiting for transfers between devices  23.3 us (22%)
  Pallas kernels  22.8 us (22%)
  between operations  1.45 us (1%)
    ppermute x26, starting transfers between devices, shift(): return lax.ppermute(value, axis, [(i, (i + by) % n) for i in range(n)])  36 us
    pallas_call x11, Pallas kernels, call(): pl.pallas_call(kernel, out_shape=[s if hasattr(s, 'dtype') else jax.Shape...  22 us
    ppermute x26, waiting for transfers between devices, shift(): return lax.ppermute(value, axis, [(i, (i + by) % n) for i in range(n)])  17.2 us
    all_to_all x1, starting transfers between devices, over_all(): return lax.all_to_all(rows, TILE + SLAB, 0, 0, tiled=True)  9.14 us
    ppermute x1, starting transfers between devices, shards(): lax.ppermute(first0, SLAB, down)  5.94 us
    ppermute x1, starting transfers between devices, shards(): lax.ppermute(first, SLAB, down)  5.46 us
    all_to_all x1, waiting for transfers between devices, over_all(): return lax.all_to_all(rows, TILE + SLAB, 0, 0, tiled=True)  4.27 us
  transfers between devices with their start and end apart: 31, of which 15 were waited for; matrix products, arithmetic and copies ran while one was open for 0% of the time, Pallas kernels for 2%

commit v1 on v0

--- a/solution.py
+++ b/solution.py
@@ -11,7 +11,7 @@
 TILE = ("tile_0", "tile_1")
 SLAB = ("slab_0", "slab_1")
 GROUP = 4
-UNROLL = 64
+UNROLL = 32
 CHUNKS = 4
 
 huber_width = 0.5
@@ -322,7 +322,10 @@
 def summed_by_owner(mine, theirs):
     got = shift(theirs, "tile_1", 1)
     kept, s1, s2, s3 = call(add_kernel, [RAY] * 4, [mine, got])
-    return kept, shift(s1, "tile_0", 1), shift(s2, "tile_0", 2), shift(s3, "tile_0", 3)
+    moved = []
+    for r, part in enumerate((s1, s2, s3), 1):
+        moved.append(shift(part, "tile_0", r))
+    return kept, *moved
 
 
 def to_everyone(own):

time: 106 us -> 105 us (level)
  no operation moved by 1% of the time
where the time goes in v1:
time: 105 us
  starting transfers between devices  57.7 us (55%)
  waiting for transfers between devices  23.2 us (22%)
  Pallas kernels  22.1 us (21%)
  between operations  1.44 us (1%)
    ppermute x26, starting transfers between devices, shift(): return lax.ppermute(value, axis, [(i, (i + by) % n) for i in range(n)])  35.9 us
    pallas_call x11, Pallas kernels, call(): pl.pallas_call(kernel, out_shape=[s if hasattr(s, 'dtype') else jax.Shape...  21.3 us
    ppermute x26, waiting for transfers between devices, shift(): return lax.ppermute(value, axis, [(i, (i + by) % n) for i in range(n)])  17.1 us
    all_to_all x1, starting transfers between devices, over_all(): return lax.all_to_all(rows, TILE + SLAB, 0, 0, tiled=True)  9.14 us
    ppermute x1, starting transfers between devices, shards(): lax.ppermute(first0, SLAB, down)  5.95 us
    ppermute x1, starting transfers between devices, shards(): lax.ppermute(first, SLAB, down)  5.46 us
    all_to_all x1, waiting for transfers between devices, over_all(): return lax.all_to_all(rows, TILE + SLAB, 0, 0, tiled=True)  4.27 us
  transfers between devices with their start and end apart: 31, of which 15 were waited for; matrix products, arithmetic and copies ran while one was open for 0% of the time, Pallas kernels for 2%

profile of v1, /device:TPU:1, one launch (start us, length us, event | category | flops | bytes accessed | tf_op | source)
XLA Modules:
  0.0 104.5 jit_solution(12489581275812006766)
XLA Ops:
  0.8 5.7 %shard_map.77 = (f32[4,8,32,128]{3,2,1,0:T(8,128)S(1)}, f32[4,8,32,128]{3,2,1,0:T(8,128)S(1)}, f32[32,8,128]{2,1,0:T(8,128)S(1)}, f32[32,8,128]{2,1,0:T(8,128)S(...) custom-call(s32[256]{0:T(256)} %pixels.3, s32[256]{0:T(256)} %strips.3, s32[2]{0:T(128)S(1)} %pad_add_fusion.me, ...), custom_call_target="tpu_custom_call" | custom-call | flops 1000000 | bytes 1048576 | tf_op jit(solution)/shard_map/pallas_call | solution.py:30
  6.5 1.5 %collective-permute-start = (f32[4,8,32,128]{3,2,1,0:T(8,128)S(1)}, f32[4,8,32,128]{3,2,1,0:T(8,128)S(1)}, u32[]{:S(2)}, u32[]{:S(2)}) collective-permute-start(f32[4,8,32,128]{3,2,1,0:T(8,128)S(1)} %get-tuple-element.78), channel_id=1, source_target_pairs={{0,16},{16,0},{1,17},{17,1},{2,18},{18,2},{3,19},{19,3},{4,20},{20... | collective-permute-start | bytes 1572872 | tf_op jit(solution)/shard_map/ppermute | solution.py:316
  8.0 1.5 %collective-permute-done.got = f32[4,8,32,128]{3,2,1,0:T(8,128)S(1)} collective-permute-done((f32[4,8,32,128]{3,2,1,0:T(8,128)S(1)}, f32[4,8,32,128]{3,2,1,0:T(8,128)S(1)}, u32[]{:S(2)}, u32[]{:S(2)}) %collective-permute-start) | collective-permute-done | bytes 524320 | tf_op jit(solution)/shard_map/ppermute | solution.py:316
  9.6 1.5 %collective-permute-start.1 = (f32[8,32,128]{2,1,0:T(8,128)S(1)}, f32[8,32,128]{2,1,0:T(8,128)S(1)}, u32[]{:S(2)}, u32[]{:S(2)}) collective-permute-start(f32[8,32,128]{2,1,0:T(8,128)S(1)} %get-tuple-element.80), channel_id=1, source_target_pairs={{0,32},{32,64},{64,96},{96,0},{1,33},{33,65},{65,97},{97,1},{2,34}... | collective-permute-start | bytes 393224 | tf_op jit(solution)/shard_map/ppermute | solution.py:316
  11.0 2.6 %collective-permute-start.2 = (f32[8,32,128]{2,1,0:T(8,128)S(1)}, f32[8,32,128]{2,1,0:T(8,128)S(1)}, u32[]{:S(2)}, u32[]{:S(2)}) collective-permute-start(f32[8,32,128]{2,1,0:T(8,128)S(1)} %get-tuple-element.81), channel_id=1, source_target_pairs={{0,64},{32,96},{64,0},{96,32},{1,65},{33,97},{65,1},{97,33},{2,66}... | collective-permute-start | bytes 393224 | tf_op jit(solution)/shard_map/ppermute | solution.py:316
  15.9 3.8 %collective-permute-done.2.b = f32[8,32,128]{2,1,0:T(8,128)S(1)} collective-permute-done((f32[8,32,128]{2,1,0:T(8,128)S(1)}, f32[8,32,128]{2,1,0:T(8,128)S(1)}, u32[]{:S(2)}, u32[]{:S(2)}) %collective-permute-start.2) | collective-permute-done | bytes 131104 | tf_op jit(solution)/shard_map/ppermute | solution.py:316
  20.8 2.3 %collective-permute-start.5 = (f32[8,32,128]{2,1,0:T(8,128)S(1)}, f32[8,32,128]{2,1,0:T(8,128)S(1)}, u32[]{:S(2)}, u32[]{:S(2)}) collective-permute-start(f32[8,32,128]{2,1,0:T(8,128)S(1)} %get-tuple-element.83.refs_0_), channel_id=1, source_target_pairs={{0,64},{32,96},{64,0},{96,32},{1,65},{33,97},{65,1},{97,33},{2,66}... | collective-permute-start | bytes 393224 | tf_op jit(solution)/shard_map/ppermute | solution.py:316
  23.9 2.3 %collective-permute-start.7 = (f32[8,32,128]{2,1,0:T(8,128)S(1)}, f32[8,32,128]{2,1,0:T(8,128)S(1)}, u32[]{:S(2)}, u32[]{:S(2)}) collective-permute-start(f32[8,32,128]{2,1,0:T(8,128)S(1)} %get-tuple-element.83.refs_0_), channel_id=1, source_target_pairs={{0,16},{16,0},{1,17},{17,1},{2,18},{18,2},{3,19},{19,3},{4,20},{20... | collective-permute-start | bytes 393224 | tf_op jit(solution)/shard_map/ppermute | solution.py:316
  26.2 2.2 %collective-permute-start.10 = (f32[8,32,128]{2,1,0:T(8,128)S(1)}, f32[8,32,128]{2,1,0:T(8,128)S(1)}, u32[]{:S(2)}, u32[]{:S(2)}) collective-permute-start(f32[8,32,128]{2,1,0:T(8,128)S(1)} %collective-permute-done.6.refs_3_), channel_id=1, source_target_pairs={{0,16},{16,0},{1,17},{17,1},{2,18},{18,2},{3,19},{19,3},{4,20},{20... | collective-permute-start | bytes 393224 | tf_op jit(solution)/shard_map/ppermute | solution.py:316
  28.4 1.9 %collective-permute-start.9 = (f32[8,32,128]{2,1,0:T(8,128)S(1)}, f32[8,32,128]{2,1,0:T(8,128)S(1)}, u32[]{:S(2)}, u32[]{:S(2)}) collective-permute-start(f32[8,32,128]{2,1,0:T(8,128)S(1)} %collective-permute-done.5.refs_2_), channel_id=1, source_target_pairs={{0,16},{16,0},{1,17},{17,1},{2,18},{18,2},{3,19},{19,3},{4,20},{20... | collective-permute-start | bytes 393224 | tf_op jit(solution)/shard_map/ppermute | solution.py:316
  31.7 5.4 %shard_map.80 = (f32[4,8,32,128]{3,2,1,0:T(8,128)S(1)}, f32[4,8,32,128]{3,2,1,0:T(8,128)S(1)}, f32[32,32,128]{2,1,0:T(8,128)S(1)}, f32[1,8,128]{2,1,0:T(8,128)S(...) custom-call(s32[256]{0:T(256)S(1)} %copy-done.2, s32[256]{0:T(256)S(1)} %copy-done.3, s32[2]{0:T(128)S(1)} %pad_add_fusion.me, ...), custom_call_target="tpu_custom_call" | custom-call | flops 1000000 | bytes 1048576 | tf_op jit(solution)/shard_map/pallas_call | solution.py:30
  37.3 1.7 %collective-permute-done.11.got = f32[4,8,32,128]{3,2,1,0:T(8,128)S(1)} collective-permute-done((f32[4,8,32,128]{3,2,1,0:T(8,128)S(1)}, f32[4,8,32,128]{3,2,1,0:T(8,128)S(1)}, u32[]{:S(2)}, u32[]{:S(2)}) %collective-permute-start.11) | collective-permute-done | bytes 524320 | tf_op jit(solution)/shard_map/ppermute | solution.py:316
  40.3 2.1 %collective-permute-start.13 = (f32[8,32,128]{2,1,0:T(8,128)S(1)}, f32[8,32,128]{2,1,0:T(8,128)S(1)}, u32[]{:S(2)}, u32[]{:S(2)}) collective-permute-start(f32[8,32,128]{2,1,0:T(8,128)S(1)} %get-tuple-element.90), channel_id=1, source_target_pairs={{0,64},{32,96},{64,0},{96,32},{1,65},{33,97},{65,1},{97,33},{2,66}... | collective-permute-start | bytes 393224 | tf_op jit(solution)/shard_map/ppermute | solution.py:316
  43.0 6.0 %collective-permute-start.22 = (f32[32,8,128]{2,1,0:T(8,128)S(1)}, f32[32,8,128]{2,1,0:T(8,128)S(1)}, u32[]{:S(2)}, u32[]{:S(2)}) collective-permute-start(f32[32,8,128]{2,1,0:T(8,128)S(1)} %get-tuple-element.92), channel_id=1, source_target_pairs={{1,0},{2,1},{3,2},{4,3},{5,4},{6,5},{7,6},{8,7},{9,8},{10,9},{11,1... | collective-permute-start | bytes 393224 | tf_op jit(solution)/shard_map/ppermute | solution.py:383
  49.0 1.4 %collective-permute-start.17 = (f32[8,32,128]{2,1,0:T(8,128)S(1)}, f32[8,32,128]{2,1,0:T(8,128)S(1)}, u32[]{:S(2)}, u32[]{:S(2)}) collective-permute-start(f32[8,32,128]{2,1,0:T(8,128)S(1)} %shard_map.82.refs_0_.sent), channel_id=1, source_target_pairs={{0,32},{32,64},{64,96},{96,0},{1,33},{33,65},{65,97},{97,1},{2,34}... | collective-permute-start | bytes 393224 | tf_op jit(solution)/shard_map/ppermute | solution.py:316
  50.4 2.4 %collective-permute-start.16 = (f32[8,32,128]{2,1,0:T(8,128)S(1)}, f32[8,32,128]{2,1,0:T(8,128)S(1)}, u32[]{:S(2)}, u32[]{:S(2)}) collective-permute-start(f32[8,32,128]{2,1,0:T(8,128)S(1)} %shard_map.82.refs_0_.sent), channel_id=1, source_target_pairs={{0,64},{32,96},{64,0},{96,32},{1,65},{33,97},{65,1},{97,33},{2,66}... | collective-permute-start | bytes 393224 | tf_op jit(solution)/shard_map/ppermute | solution.py:316
  52.9 1.2 %collective-permute-start.23 = (f32[32,8,128]{2,1,0:T(8,128)S(1)}, f32[32,8,128]{2,1,0:T(8,128)S(1)}, u32[]{:S(2)}, u32[]{:S(2)}) collective-permute-start(f32[32,8,128]{2,1,0:T(8,128)S(1)} %get-tuple-element.93), channel_id=1, source_target_pairs={{0,1},{1,2},{2,3},{3,4},{4,5},{5,6},{6,7},{7,8},{8,9},{9,10},{10,1... | collective-permute-start | bytes 393224 | tf_op jit(solution)/shard_map/ppermute | solution.py:383
  54.1 1.8 %collective-permute-start.18 = (f32[8,32,128]{2,1,0:T(8,128)S(1)}, f32[8,32,128]{2,1,0:T(8,128)S(1)}, u32[]{:S(2)}, u32[]{:S(2)}) collective-permute-start(f32[8,32,128]{2,1,0:T(8,128)S(1)} %shard_map.82.refs_0_.sent), channel_id=1, source_target_pairs={{0,16},{16,0},{1,17},{17,1},{2,18},{18,2},{3,19},{19,3},{4,20},{20... | collective-permute-start | bytes 393224 | tf_op jit(solution)/shard_map/ppermute | solution.py:316
  55.9 1.3 %collective-permute-start.21 = (f32[8,32,128]{2,1,0:T(8,128)S(1)}, f32[8,32,128]{2,1,0:T(8,128)S(1)}, u32[]{:S(2)}, u32[]{:S(2)}) collective-permute-start(f32[8,32,128]{2,1,0:T(8,128)S(1)} %collective-permute-done.17.refs_3_), channel_id=1, source_target_pairs={{0,16},{16,0},{1,17},{17,1},{2,18},{18,2},{3,19},{19,3},{4,20},{20... | collective-permute-start | bytes 393224 | tf_op jit(solution)/shard_map/ppermute | solution.py:316
  57.2 1.5 %collective-permute-done.16.refs_2_ = f32[8,32,128]{2,1,0:T(8,128)S(1)} collective-permute-done((f32[8,32,128]{2,1,0:T(8,128)S(1)}, f32[8,32,128]{2,1,0:T(8,128)S(1)}, u32[]{:S(2)}, u32[]{:S(2)}) %collective-permute-start.16) | collective-permute-done | bytes 131104 | tf_op jit(solution)/shard_map/ppermute | solution.py:316
  58.7 1.4 %collective-permute-start.20 = (f32[8,32,128]{2,1,0:T(8,128)S(1)}, f32[8,32,128]{2,1,0:T(8,128)S(1)}, u32[]{:S(2)}, u32[]{:S(2)}) collective-permute-start(f32[8,32,128]{2,1,0:T(8,128)S(1)} %collective-permute-done.16.refs_2_), channel_id=1, source_target_pairs={{0,16},{16,0},{1,17},{17,1},{2,18},{18,2},{3,19},{19,3},{4,20},{20... | collective-permute-start | bytes 393224 | tf_op jit(solution)/shard_map/ppermute | solution.py:316
  61.4 5.4 %shard_map.83 = (f32[4,8,32,128]{3,2,1,0:T(8,128)S(1)}, f32[4,8,32,128]{3,2,1,0:T(8,128)S(1)}, f32[32,32,128]{2,1,0:T(8,128)S(1)}, f32[2,8,128]{2,1,0:T(8,128)S(...) custom-call(s32[256]{0:T(256)S(1)} %copy-done.2, s32[256]{0:T(256)S(1)} %copy-done.3, s32[2]{0:T(128)S(1)} %pad_add_fusion.me, ...), custom_call_target="tpu_custom_call" | custom-call | flops 1000000 | bytes 1048576 | tf_op jit(solution)/shard_map/pallas_call | solution.py:30
  66.9 2.3 %collective-permute-start.24 = (f32[4,8,32,128]{3,2,1,0:T(8,128)S(1)}, f32[4,8,32,128]{3,2,1,0:T(8,128)S(1)}, u32[]{:S(2)}, u32[]{:S(2)}) collective-permute-start(f32[4,8,32,128]{3,2,1,0:T(8,128)S(1)} %get-tuple-element.104), channel_id=1, source_target_pairs={{0,16},{16,0},{1,17},{17,1},{2,18},{18,2},{3,19},{19,3},{4,20},{20... | collective-permute-start | bytes 1572872 | tf_op jit(solution)/shard_map/ppermute | solution.py:316
  69.2 1.5 %collective-permute-done.24.got = f32[4,8,32,128]{3,2,1,0:T(8,128)S(1)} collective-permute-done((f32[4,8,32,128]{3,2,1,0:T(8,128)S(1)}, f32[4,8,32,128]{3,2,1,0:T(8,128)S(1)}, u32[]{:S(2)}, u32[]{:S(2)}) %collective-permute-start.24) | collective-permute-done | bytes 524320 | tf_op jit(solution)/shard_map/ppermute | solution.py:316
  70.8 1.3 %collective-permute-start.25 = (f32[8,32,128]{2,1,0:T(8,128)S(1)}, f32[8,32,128]{2,1,0:T(8,128)S(1)}, u32[]{:S(2)}, u32[]{:S(2)}) collective-permute-start(f32[8,32,128]{2,1,0:T(8,128)S(1)} %get-tuple-element.106), channel_id=1, source_target_pairs={{0,32},{32,64},{64,96},{96,0},{1,33},{33,65},{65,97},{97,1},{2,34}... | collective-permute-start | bytes 393224 | tf_op jit(solution)/shard_map/ppermute | solution.py:316
  72.6 2.0 %collective-permute-start.27 = (f32[8,32,128]{2,1,0:T(8,128)S(1)}, f32[8,32,128]{2,1,0:T(8,128)S(1)}, u32[]{:S(2)}, u32[]{:S(2)}) collective-permute-start(f32[8,32,128]{2,1,0:T(8,128)S(1)} %get-tuple-element.108), channel_id=1, source_target_pairs={{0,96},{32,0},{64,32},{96,64},{1,97},{33,1},{65,33},{97,65},{2,98}... | collective-permute-start | bytes 393224 | tf_op jit(solution)/shard_map/ppermute | solution.py:316
  75.5 1.5 %collective-permute-done.25.a = f32[8,32,128]{2,1,0:T(8,128)S(1)} collective-permute-done((f32[8,32,128]{2,1,0:T(8,128)S(1)}, f32[8,32,128]{2,1,0:T(8,128)S(1)}, u32[]{:S(2)}, u32[]{:S(2)}) %collective-permute-start.25) | collective-permute-done | bytes 131104 | tf_op jit(solution)/shard_map/ppermute | solution.py:316
  77.1 1.6 %collective-permute-done.26.b = f32[8,32,128]{2,1,0:T(8,128)S(1)} collective-permute-done((f32[8,32,128]{2,1,0:T(8,128)S(1)}, f32[8,32,128]{2,1,0:T(8,128)S(1)}, u32[]{:S(2)}, u32[]{:S(2)}) %collective-permute-start.26) | collective-permute-done | bytes 131104 | tf_op jit(solution)/shard_map/ppermute | solution.py:316
  80.8 9.1 %all-to-all-start.1 = ((f32[128,1,128]{2,1,0:T(1,128)}), f32[128,1,128]{2,1,0:T(1,128)S(1)}, u32[]{:S(2)}, u32[]{:S(2)}) async-start(f32[128,1,128]{2,1,0:T(1,128)} %bitcast.9), calls=%async_computation.1 | async-start | bytes 131072 | tf_op jit(solution)/shard_map/all_to_all | solution.py:337
  89.9 5.5 %collective-permute-start.28 = (f32[16,8,128]{2,1,0:T(8,128)S(1)}, f32[16,8,128]{2,1,0:T(8,128)S(1)}, u32[]{:S(2)}, u32[]{:S(2)}) collective-permute-start(f32[16,8,128]{2,1,0:T(8,128)S(1)} %get-tuple-element.123), channel_id=1, source_target_pairs={{1,0},{2,1},{3,2},{4,3},{5,4},{6,5},{7,6},{8,7},{9,8},{10,9},{11,1... | collective-permute-start | bytes 196616 | tf_op jit(solution)/shard_map/ppermute | solution.py:398
  95.4 4.3 %all-to-all-done.1 = f32[128,1,128]{2,1,0:T(1,128)S(1)} async-done(((f32[128,1,128]{2,1,0:T(1,128)}), f32[128,1,128]{2,1,0:T(1,128)S(1)}, u32[]{:S(2)}, u32[]{:S(2)}) %all-to-all-start.1) | async-done | bytes 65568 | tf_op jit(solution)/shard_map/all_to_all | solution.py:337
  101.8 2.7 %shard_map.88 = (f32[32,4096]{1,0:T(8,128)}, f32[32,1024]{1,0:T(8,128)}) custom-call(s32[2]{0:T(128)S(1)} %add_convert_fusion.ends, f32[2]{0:T(128)S(1)} %get-tuple-element.126.alphas, f32[32,4096]{1,0:T(8,128)S(1)} %copy-done, f32[32,32,128]{2,1,0:T(8,128)} %copy-done.4, f32[32,32,128]{2,1,0:T(8,128)S(1)} %get-tuple-element.109.back.turned, ...), custom_call_target="tpu_custom_call" | custom-call | flops 1000000 | bytes 1048576 | tf_op jit(solution)/shard_map/pallas_call | solution.py:30
  (57 shorter events, 14.2 us)
Async XLA Ops:
  6.5 3.0 %collective-permute-start = (f32[4,8,32,128]{3,2,1,0:T(8,128)S(1)}, f32[4,8,32,128]{3,2,1,0:T(8,128)S(1)}, u32[]{:S(2)}, u32[]{:S(2)}) collective-permute-start(f32[4,8,32,128]{3,2,1,0:T(8,128)S(1)} %get-tuple-element.78), channel_id=1, source_target_pairs={{0,16},{16,0},{1,17},{17,1},{2,18},{18,2},{3,19},{19,3},{4,20},{20... | collective-permute-start | bytes 1572872 | tf_op jit(solution)/shard_map/ppermute | solution.py:316
  9.6 6.3 %collective-permute-start.1 = (f32[8,32,128]{2,1,0:T(8,128)S(1)}, f32[8,32,128]{2,1,0:T(8,128)S(1)}, u32[]{:S(2)}, u32[]{:S(2)}) collective-permute-start(f32[8,32,128]{2,1,0:T(8,128)S(1)} %get-tuple-element.80), channel_id=1, source_target_pairs={{0,32},{32,64},{64,96},{96,0},{1,33},{33,65},{65,97},{97,1},{2,34}... | collective-permute-start | bytes 393224 | tf_op jit(solution)/shard_map/ppermute | solution.py:316
  11.0 8.7 %collective-permute-start.2 = (f32[8,32,128]{2,1,0:T(8,128)S(1)}, f32[8,32,128]{2,1,0:T(8,128)S(1)}, u32[]{:S(2)}, u32[]{:S(2)}) collective-permute-start(f32[8,32,128]{2,1,0:T(8,128)S(1)} %get-tuple-element.81), channel_id=1, source_target_pairs={{0,64},{32,96},{64,0},{96,32},{1,65},{33,97},{65,1},{97,33},{2,66}... | collective-permute-start | bytes 393224 | tf_op jit(solution)/shard_map/ppermute | solution.py:316
  13.6 6.0 %collective-permute-start.3 = (f32[8,32,128]{2,1,0:T(8,128)S(1)}, f32[8,32,128]{2,1,0:T(8,128)S(1)}, u32[]{:S(2)}, u32[]{:S(2)}) collective-permute-start(f32[8,32,128]{2,1,0:T(8,128)S(1)} %get-tuple-element.82), channel_id=1, source_target_pairs={{0,96},{32,0},{64,32},{96,64},{1,97},{33,1},{65,33},{97,65},{2,98}... | collective-permute-start | bytes 393224 | tf_op jit(solution)/shard_map/ppermute | solution.py:316
  19.7 6.5 %collective-permute-start.6 = (f32[8,32,128]{2,1,0:T(8,128)S(1)}, f32[8,32,128]{2,1,0:T(8,128)S(1)}, u32[]{:S(2)}, u32[]{:S(2)}) collective-permute-start(f32[8,32,128]{2,1,0:T(8,128)S(1)} %get-tuple-element.83.refs_0_), channel_id=1, source_target_pairs={{0,32},{32,64},{64,96},{96,0},{1,33},{33,65},{65,97},{97,1},{2,34}... | collective-permute-start | bytes 393224 | tf_op jit(solution)/shard_map/ppermute | solution.py:316
  20.8 7.6 %collective-permute-start.5 = (f32[8,32,128]{2,1,0:T(8,128)S(1)}, f32[8,32,128]{2,1,0:T(8,128)S(1)}, u32[]{:S(2)}, u32[]{:S(2)}) collective-permute-start(f32[8,32,128]{2,1,0:T(8,128)S(1)} %get-tuple-element.83.refs_0_), channel_id=1, source_target_pairs={{0,64},{32,96},{64,0},{96,32},{1,65},{33,97},{65,1},{97,33},{2,66}... | collective-permute-start | bytes 393224 | tf_op jit(solution)/shard_map/ppermute | solution.py:316
  23.0 7.3 %collective-permute-start.4 = (f32[8,32,128]{2,1,0:T(8,128)S(1)}, f32[8,32,128]{2,1,0:T(8,128)S(1)}, u32[]{:S(2)}, u32[]{:S(2)}) collective-permute-start(f32[8,32,128]{2,1,0:T(8,128)S(1)} %get-tuple-element.83.refs_0_), channel_id=1, source_target_pairs={{0,96},{32,0},{64,32},{96,64},{1,97},{33,1},{65,33},{97,65},{2,98}... | collective-permute-start | bytes 393224 | tf_op jit(solution)/shard_map/ppermute | solution.py:316
  23.9 6.4 %collective-permute-start.7 = (f32[8,32,128]{2,1,0:T(8,128)S(1)}, f32[8,32,128]{2,1,0:T(8,128)S(1)}, u32[]{:S(2)}, u32[]{:S(2)}) collective-permute-start(f32[8,32,128]{2,1,0:T(8,128)S(1)} %get-tuple-element.83.refs_0_), channel_id=1, source_target_pairs={{0,16},{16,0},{1,17},{17,1},{2,18},{18,2},{3,19},{19,3},{4,20},{20... | collective-permute-start | bytes 393224 | tf_op jit(solution)/shard_map/ppermute | solution.py:316
  26.2 4.1 %collective-permute-start.10 = (f32[8,32,128]{2,1,0:T(8,128)S(1)}, f32[8,32,128]{2,1,0:T(8,128)S(1)}, u32[]{:S(2)}, u32[]{:S(2)}) collective-permute-start(f32[8,32,128]{2,1,0:T(8,128)S(1)} %collective-permute-done.6.refs_3_), channel_id=1, source_target_pairs={{0,16},{16,0},{1,17},{17,1},{2,18},{18,2},{3,19},{19,3},{4,20},{20... | collective-permute-start | bytes 393224 | tf_op jit(solution)/shard_map/ppermute | solution.py:316
  28.4 2.9 %collective-permute-start.9 = (f32[8,32,128]{2,1,0:T(8,128)S(1)}, f32[8,32,128]{2,1,0:T(8,128)S(1)}, u32[]{:S(2)}, u32[]{:S(2)}) collective-permute-start(f32[8,32,128]{2,1,0:T(8,128)S(1)} %collective-permute-done.5.refs_2_), channel_id=1, source_target_pairs={{0,16},{16,0},{1,17},{17,1},{2,18},{18,2},{3,19},{19,3},{4,20},{20... | collective-permute-start | bytes 393224 | tf_op jit(solution)/shard_map/ppermute | solution.py:316
  30.3 1.3 %collective-permute-start.8 = (f32[8,32,128]{2,1,0:T(8,128)S(1)}, f32[8,32,128]{2,1,0:T(8,128)S(1)}, u32[]{:S(2)}, u32[]{:S(2)}) collective-permute-start(f32[8,32,128]{2,1,0:T(8,128)S(1)} %collective-permute-done.4.refs_1_), channel_id=1, source_target_pairs={{0,16},{16,0},{1,17},{17,1},{2,18},{18,2},{3,19},{19,3},{4,20},{20... | collective-permute-start | bytes 393224 | tf_op jit(solution)/shard_map/ppermute | solution.py:316
  37.1 2.0 %collective-permute-start.11 = (f32[4,8,32,128]{3,2,1,0:T(8,128)S(1)}, f32[4,8,32,128]{3,2,1,0:T(8,128)S(1)}, u32[]{:S(2)}, u32[]{:S(2)}) collective-permute-start(f32[4,8,32,128]{3,2,1,0:T(8,128)S(1)} %get-tuple-element.87), channel_id=1, source_target_pairs={{0,16},{16,0},{1,17},{17,1},{2,18},{18,2},{3,19},{19,3},{4,20},{20... | collective-permute-start | bytes 1572872 | tf_op jit(solution)/shard_map/ppermute | solution.py:316
  39.1 9.8 %collective-permute-start.12 = (f32[8,32,128]{2,1,0:T(8,128)S(1)}, f32[8,32,128]{2,1,0:T(8,128)S(1)}, u32[]{:S(2)}, u32[]{:S(2)}) collective-permute-start(f32[8,32,128]{2,1,0:T(8,128)S(1)} %get-tuple-element.89), channel_id=1, source_target_pairs={{0,32},{32,64},{64,96},{96,0},{1,33},{33,65},{65,97},{97,1},{2,34}... | collective-permute-start | bytes 393224 | tf_op jit(solution)/shard_map/ppermute | solution.py:316
  40.3 8.6 %collective-permute-start.13 = (f32[8,32,128]{2,1,0:T(8,128)S(1)}, f32[8,32,128]{2,1,0:T(8,128)S(1)}, u32[]{:S(2)}, u32[]{:S(2)}) collective-permute-start(f32[8,32,128]{2,1,0:T(8,128)S(1)} %get-tuple-element.90), channel_id=1, source_target_pairs={{0,64},{32,96},{64,0},{96,32},{1,65},{33,97},{65,1},{97,33},{2,66}... | collective-permute-start | bytes 393224 | tf_op jit(solution)/shard_map/ppermute | solution.py:316
  42.4 6.5 %collective-permute-start.14 = (f32[8,32,128]{2,1,0:T(8,128)S(1)}, f32[8,32,128]{2,1,0:T(8,128)S(1)}, u32[]{:S(2)}, u32[]{:S(2)}) collective-permute-start(f32[8,32,128]{2,1,0:T(8,128)S(1)} %get-tuple-element.91), channel_id=1, source_target_pairs={{0,96},{32,0},{64,32},{96,64},{1,97},{33,1},{65,33},{97,65},{2,98}... | collective-permute-start | bytes 393224 | tf_op jit(solution)/shard_map/ppermute | solution.py:316
  43.0 11.1 %collective-permute-start.22 = (f32[32,8,128]{2,1,0:T(8,128)S(1)}, f32[32,8,128]{2,1,0:T(8,128)S(1)}, u32[]{:S(2)}, u32[]{:S(2)}) collective-permute-start(f32[32,8,128]{2,1,0:T(8,128)S(1)} %get-tuple-element.92), channel_id=1, source_target_pairs={{1,0},{2,1},{3,2},{4,3},{5,4},{6,5},{7,6},{8,7},{9,8},{10,9},{11,1... | collective-permute-start | bytes 393224 | tf_op jit(solution)/shard_map/ppermute | solution.py:383
  49.0 6.9 %collective-permute-start.17 = (f32[8,32,128]{2,1,0:T(8,128)S(1)}, f32[8,32,128]{2,1,0:T(8,128)S(1)}, u32[]{:S(2)}, u32[]{:S(2)}) collective-permute-start(f32[8,32,128]{2,1,0:T(8,128)S(1)} %shard_map.82.refs_0_.sent), channel_id=1, source_target_pairs={{0,32},{32,64},{64,96},{96,0},{1,33},{33,65},{65,97},{97,1},{2,34}... | collective-permute-start | bytes 393224 | tf_op jit(solution)/shard_map/ppermute | solution.py:316
  50.4 8.2 %collective-permute-start.16 = (f32[8,32,128]{2,1,0:T(8,128)S(1)}, f32[8,32,128]{2,1,0:T(8,128)S(1)}, u32[]{:S(2)}, u32[]{:S(2)}) collective-permute-start(f32[8,32,128]{2,1,0:T(8,128)S(1)} %shard_map.82.refs_0_.sent), channel_id=1, source_target_pairs={{0,64},{32,96},{64,0},{96,32},{1,65},{33,97},{65,1},{97,33},{2,66}... | collective-permute-start | bytes 393224 | tf_op jit(solution)/shard_map/ppermute | solution.py:316
  52.8 7.3 %collective-permute-start.15 = (f32[8,32,128]{2,1,0:T(8,128)S(1)}, f32[8,32,128]{2,1,0:T(8,128)S(1)}, u32[]{:S(2)}, u32[]{:S(2)}) collective-permute-start(f32[8,32,128]{2,1,0:T(8,128)S(1)} %shard_map.82.refs_0_.sent), channel_id=1, source_target_pairs={{0,96},{32,0},{64,32},{96,64},{1,97},{33,1},{65,33},{97,65},{2,98}... | collective-permute-start | bytes 393224 | tf_op jit(solution)/shard_map/ppermute | solution.py:316
  52.9 8.3 %collective-permute-start.23 = (f32[32,8,128]{2,1,0:T(8,128)S(1)}, f32[32,8,128]{2,1,0:T(8,128)S(1)}, u32[]{:S(2)}, u32[]{:S(2)}) collective-permute-start(f32[32,8,128]{2,1,0:T(8,128)S(1)} %get-tuple-element.93), channel_id=1, source_target_pairs={{0,1},{1,2},{2,3},{3,4},{4,5},{5,6},{6,7},{7,8},{8,9},{9,10},{10,1... | collective-permute-start | bytes 393224 | tf_op jit(solution)/shard_map/ppermute | solution.py:383
  54.1 7.1 %collective-permute-start.18 = (f32[8,32,128]{2,1,0:T(8,128)S(1)}, f32[8,32,128]{2,1,0:T(8,128)S(1)}, u32[]{:S(2)}, u32[]{:S(2)}) collective-permute-start(f32[8,32,128]{2,1,0:T(8,128)S(1)} %shard_map.82.refs_0_.sent), channel_id=1, source_target_pairs={{0,16},{16,0},{1,17},{17,1},{2,18},{18,2},{3,19},{19,3},{4,20},{20... | collective-permute-start | bytes 393224 | tf_op jit(solution)/shard_map/ppermute | solution.py:316
  55.9 5.3 %collective-permute-start.21 = (f32[8,32,128]{2,1,0:T(8,128)S(1)}, f32[8,32,128]{2,1,0:T(8,128)S(1)}, u32[]{:S(2)}, u32[]{:S(2)}) collective-permute-start(f32[8,32,128]{2,1,0:T(8,128)S(1)} %collective-permute-done.17.refs_3_), channel_id=1, source_target_pairs={{0,16},{16,0},{1,17},{17,1},{2,18},{18,2},{3,19},{19,3},{4,20},{20... | collective-permute-start | bytes 393224 | tf_op jit(solution)/shard_map/ppermute | solution.py:316
  58.7 2.6 %collective-permute-start.20 = (f32[8,32,128]{2,1,0:T(8,128)S(1)}, f32[8,32,128]{2,1,0:T(8,128)S(1)}, u32[]{:S(2)}, u32[]{:S(2)}) collective-permute-start(f32[8,32,128]{2,1,0:T(8,128)S(1)} %collective-permute-done.16.refs_2_), channel_id=1, source_target_pairs={{0,16},{16,0},{1,17},{17,1},{2,18},{18,2},{3,19},{19,3},{4,20},{20... | collective-permute-start | bytes 393224 | tf_op jit(solution)/shard_map/ppermute | solution.py:316
  60.1 1.3 %collective-permute-start.19 = (f32[8,32,128]{2,1,0:T(8,128)S(1)}, f32[8,32,128]{2,1,0:T(8,128)S(1)}, u32[]{:S(2)}, u32[]{:S(2)}) collective-permute-start(f32[8,32,128]{2,1,0:T(8,128)S(1)} %collective-permute-done.15.refs_1_), channel_id=1, source_target_pairs={{0,16},{16,0},{1,17},{17,1},{2,18},{18,2},{3,19},{19,3},{4,20},{20... | collective-permute-start | bytes 393224 | tf_op jit(solution)/shard_map/ppermute | solution.py:316
  66.9 34.9 %copy-start = (f32[32,4096]{1,0:T(8,128)S(1)}, f32[32,4096]{1,0:T(8,128)}, u32[]{:S(2)}) copy-start(f32[32,4096]{1,0:T(8,128)} %volume.1) | copy-start | bytes 1572868
  66.9 3.8 %collective-permute-start.24 = (f32[4,8,32,128]{3,2,1,0:T(8,128)S(1)}, f32[4,8,32,128]{3,2,1,0:T(8,128)S(1)}, u32[]{:S(2)}, u32[]{:S(2)}) collective-permute-start(f32[4,8,32,128]{3,2,1,0:T(8,128)S(1)} %get-tuple-element.104), channel_id=1, source_target_pairs={{0,16},{16,0},{1,17},{17,1},{2,18},{18,2},{3,19},{19,3},{4,20},{20... | collective-permute-start | bytes 1572872 | tf_op jit(solution)/shard_map/ppermute | solution.py:316
  70.8 6.3 %collective-permute-start.25 = (f32[8,32,128]{2,1,0:T(8,128)S(1)}, f32[8,32,128]{2,1,0:T(8,128)S(1)}, u32[]{:S(2)}, u32[]{:S(2)}) collective-permute-start(f32[8,32,128]{2,1,0:T(8,128)S(1)} %get-tuple-element.106), channel_id=1, source_target_pairs={{0,32},{32,64},{64,96},{96,0},{1,33},{33,65},{65,97},{97,1},{2,34}... | collective-permute-start | bytes 393224 | tf_op jit(solution)/shard_map/ppermute | solution.py:316
  72.1 6.6 %collective-permute-start.26 = (f32[8,32,128]{2,1,0:T(8,128)S(1)}, f32[8,32,128]{2,1,0:T(8,128)S(1)}, u32[]{:S(2)}, u32[]{:S(2)}) collective-permute-start(f32[8,32,128]{2,1,0:T(8,128)S(1)} %get-tuple-element.107), channel_id=1, source_target_pairs={{0,64},{32,96},{64,0},{96,32},{1,65},{33,97},{65,1},{97,33},{2,66}... | collective-permute-start | bytes 393224 | tf_op jit(solution)/shard_map/ppermute | solution.py:316
  72.6 7.2 %collective-permute-start.27 = (f32[8,32,128]{2,1,0:T(8,128)S(1)}, f32[8,32,128]{2,1,0:T(8,128)S(1)}, u32[]{:S(2)}, u32[]{:S(2)}) collective-permute-start(f32[8,32,128]{2,1,0:T(8,128)S(1)} %get-tuple-element.108), channel_id=1, source_target_pairs={{0,96},{32,0},{64,32},{96,64},{1,97},{33,1},{65,33},{97,65},{2,98}... | collective-permute-start | bytes 393224 | tf_op jit(solution)/shard_map/ppermute | solution.py:316
  80.8 18.9 %all-to-all-start.1 = ((f32[128,1,128]{2,1,0:T(1,128)}), f32[128,1,128]{2,1,0:T(1,128)S(1)}, u32[]{:S(2)}, u32[]{:S(2)}) async-start(f32[128,1,128]{2,1,0:T(1,128)} %bitcast.9), calls=%async_computation.1 | async-start | bytes 131072 | tf_op jit(solution)/shard_map/all_to_all | solution.py:337
  89.9 11.2 %collective-permute-start.28 = (f32[16,8,128]{2,1,0:T(8,128)S(1)}, f32[16,8,128]{2,1,0:T(8,128)S(1)}, u32[]{:S(2)}, u32[]{:S(2)}) collective-permute-start(f32[16,8,128]{2,1,0:T(8,128)S(1)} %get-tuple-element.123), channel_id=1, source_target_pairs={{1,0},{2,1},{3,2},{4,3},{5,4},{6,5},{7,6},{8,7},{9,8},{10,9},{11,1... | collective-permute-start | bytes 196616 | tf_op jit(solution)/shard_map/ppermute | solution.py:398
  95.4 6.4 %collective-permute-start.29 = (f32[16,8,128]{2,1,0:T(8,128)S(1)}, f32[16,8,128]{2,1,0:T(8,128)S(1)}, u32[]{:S(2)}, u32[]{:S(2)}) collective-permute-start(f32[16,8,128]{2,1,0:T(8,128)S(1)} %get-tuple-element.124), channel_id=1, source_target_pairs={{0,1},{1,2},{2,3},{3,4},{4,5},{5,6},{6,7},{7,8},{8,9},{9,10},{10,1... | collective-permute-start | bytes 196616 | tf_op jit(solution)/shard_map/ppermute | solution.py:398
  (5 other events, 129.9 us)

commit v2 on v1

--- a/solution.py
+++ b/solution.py
@@ -329,7 +329,9 @@
 
 
 def to_everyone(own):
-    column = [own] + [shift(own, "tile_0", -r) for r in (1, 2, 3)]
+    column = [own]
+    for r in (1, 2, 3):
+        column.append(shift(own, "tile_0", -r))
     return column + [shift(block, "tile_1", 1) for block in column]
 
 
@@ -372,10 +374,11 @@
     parts = summed_by_owner(mine, theirs)
     residual, sent = call(start_kernel, [RAY, RAY], [*parts, measured, weights])
 
+    pieces = to_everyone(sent)
     mine, theirs, grad, norm0, first0, last0 = call(
         second_kernel,
         [half, half, field, tile, edge, edge],
-        [*spots, plain, turned, *to_everyone(sent), first0, last0],
+        [*spots, plain, turned, *pieces, first0, last0],
         scratch,
         3,
     )

time: 105 us -> 105 us (level)
  no operation moved by 1% of the time
where the time goes in v2:
time: 105 us
  starting transfers between devices  57.7 us (55%)
  waiting for transfers between devices  23.2 us (22%)
  Pallas kernels  22.1 us (21%)
  between operations  1.44 us (1%)
    ppermute x26, starting transfers between devices, shift(): return lax.ppermute(value, axis, [(i, (i + by) % n) for i in range(n)])  35.9 us
    pallas_call x11, Pallas kernels, call(): pl.pallas_call(kernel, out_shape=[s if hasattr(s, 'dtype') else jax.Shape...  21.3 us
    ppermute x26, waiting for transfers between devices, shift(): return lax.ppermute(value, axis, [(i, (i + by) % n) for i in range(n)])  17.1 us
    all_to_all x1, starting transfers between devices, over_all(): return lax.all_to_all(rows, TILE + SLAB, 0, 0, tiled=True)  9.14 us
    ppermute x1, starting transfers between devices, shards(): lax.ppermute(first0, SLAB, down)  5.95 us
    ppermute x1, starting transfers between devices, shards(): lax.ppermute(first, SLAB, down)  5.46 us
    all_to_all x1, waiting for transfers between devices, over_all(): return lax.all_to_all(rows, TILE + SLAB, 0, 0, tiled=True)  4.27 us
  transfers between devices with their start and end apart: 31, of which 15 were waited for; matrix products, arithmetic and copies ran while one was open for 0% of the time, Pallas kernels for 2%

profile of v2, /device:TPU:1, one launch (start us, length us, event | category | flops | bytes accessed | tf_op | source)
XLA Modules:
  0.0 104.5 jit_solution(12489581275812006766)
XLA Ops:
  0.8 5.7 %shard_map.77 = (f32[4,8,32,128]{3,2,1,0:T(8,128)S(1)}, f32[4,8,32,128]{3,2,1,0:T(8,128)S(1)}, f32[32,8,128]{2,1,0:T(8,128)S(1)}, f32[32,8,128]{2,1,0:T(8,128)S(...) custom-call(s32[256]{0:T(256)} %pixels.3, s32[256]{0:T(256)} %strips.3, s32[2]{0:T(128)S(1)} %pad_add_fusion.me, ...), custom_call_target="tpu_custom_call" | custom-call | flops 1000000 | bytes 1048576 | tf_op jit(solution)/shard_map/pallas_call | solution.py:30
  6.5 1.5 %collective-permute-start = (f32[4,8,32,128]{3,2,1,0:T(8,128)S(1)}, f32[4,8,32,128]{3,2,1,0:T(8,128)S(1)}, u32[]{:S(2)}, u32[]{:S(2)}) collective-permute-start(f32[4,8,32,128]{3,2,1,0:T(8,128)S(1)} %get-tuple-element.78), channel_id=1, source_target_pairs={{0,16},{16,0},{1,17},{17,1},{2,18},{18,2},{3,19},{19,3},{4,20},{20... | collective-permute-start | bytes 1572872 | tf_op jit(solution)/shard_map/ppermute | solution.py:316
  8.0 1.5 %collective-permute-done.got = f32[4,8,32,128]{3,2,1,0:T(8,128)S(1)} collective-permute-done((f32[4,8,32,128]{3,2,1,0:T(8,128)S(1)}, f32[4,8,32,128]{3,2,1,0:T(8,128)S(1)}, u32[]{:S(2)}, u32[]{:S(2)}) %collective-permute-start) | collective-permute-done | bytes 524320 | tf_op jit(solution)/shard_map/ppermute | solution.py:316
  9.6 1.5 %collective-permute-start.1 = (f32[8,32,128]{2,1,0:T(8,128)S(1)}, f32[8,32,128]{2,1,0:T(8,128)S(1)}, u32[]{:S(2)}, u32[]{:S(2)}) collective-permute-start(f32[8,32,128]{2,1,0:T(8,128)S(1)} %get-tuple-element.80), channel_id=1, source_target_pairs={{0,32},{32,64},{64,96},{96,0},{1,33},{33,65},{65,97},{97,1},{2,34}... | collective-permute-start | bytes 393224 | tf_op jit(solution)/shard_map/ppermute | solution.py:316
  11.0 2.6 %collective-permute-start.2 = (f32[8,32,128]{2,1,0:T(8,128)S(1)}, f32[8,32,128]{2,1,0:T(8,128)S(1)}, u32[]{:S(2)}, u32[]{:S(2)}) collective-permute-start(f32[8,32,128]{2,1,0:T(8,128)S(1)} %get-tuple-element.81), channel_id=1, source_target_pairs={{0,64},{32,96},{64,0},{96,32},{1,65},{33,97},{65,1},{97,33},{2,66}... | collective-permute-start | bytes 393224 | tf_op jit(solution)/shard_map/ppermute | solution.py:316
  15.9 3.8 %collective-permute-done.2.b = f32[8,32,128]{2,1,0:T(8,128)S(1)} collective-permute-done((f32[8,32,128]{2,1,0:T(8,128)S(1)}, f32[8,32,128]{2,1,0:T(8,128)S(1)}, u32[]{:S(2)}, u32[]{:S(2)}) %collective-permute-start.2) | collective-permute-done | bytes 131104 | tf_op jit(solution)/shard_map/ppermute | solution.py:316
  20.8 2.3 %collective-permute-start.5 = (f32[8,32,128]{2,1,0:T(8,128)S(1)}, f32[8,32,128]{2,1,0:T(8,128)S(1)}, u32[]{:S(2)}, u32[]{:S(2)}) collective-permute-start(f32[8,32,128]{2,1,0:T(8,128)S(1)} %get-tuple-element.83.refs_0_), channel_id=1, source_target_pairs={{0,64},{32,96},{64,0},{96,32},{1,65},{33,97},{65,1},{97,33},{2,66}... | collective-permute-start | bytes 393224 | tf_op jit(solution)/shard_map/ppermute | solution.py:316
  23.9 2.3 %collective-permute-start.7 = (f32[8,32,128]{2,1,0:T(8,128)S(1)}, f32[8,32,128]{2,1,0:T(8,128)S(1)}, u32[]{:S(2)}, u32[]{:S(2)}) collective-permute-start(f32[8,32,128]{2,1,0:T(8,128)S(1)} %get-tuple-element.83.refs_0_), channel_id=1, source_target_pairs={{0,16},{16,0},{1,17},{17,1},{2,18},{18,2},{3,19},{19,3},{4,20},{20... | collective-permute-start | bytes 393224 | tf_op jit(solution)/shard_map/ppermute | solution.py:316
  26.2 2.2 %collective-permute-start.10 = (f32[8,32,128]{2,1,0:T(8,128)S(1)}, f32[8,32,128]{2,1,0:T(8,128)S(1)}, u32[]{:S(2)}, u32[]{:S(2)}) collective-permute-start(f32[8,32,128]{2,1,0:T(8,128)S(1)} %collective-permute-done.6.refs_3_), channel_id=1, source_target_pairs={{0,16},{16,0},{1,17},{17,1},{2,18},{18,2},{3,19},{19,3},{4,20},{20... | collective-permute-start | bytes 393224 | tf_op jit(solution)/shard_map/ppermute | solution.py:316
  28.4 1.9 %collective-permute-start.9 = (f32[8,32,128]{2,1,0:T(8,128)S(1)}, f32[8,32,128]{2,1,0:T(8,128)S(1)}, u32[]{:S(2)}, u32[]{:S(2)}) collective-permute-start(f32[8,32,128]{2,1,0:T(8,128)S(1)} %collective-permute-done.5.refs_2_), channel_id=1, source_target_pairs={{0,16},{16,0},{1,17},{17,1},{2,18},{18,2},{3,19},{19,3},{4,20},{20... | collective-permute-start | bytes 393224 | tf_op jit(solution)/shard_map/ppermute | solution.py:316
  31.7 5.4 %shard_map.80 = (f32[4,8,32,128]{3,2,1,0:T(8,128)S(1)}, f32[4,8,32,128]{3,2,1,0:T(8,128)S(1)}, f32[32,32,128]{2,1,0:T(8,128)S(1)}, f32[1,8,128]{2,1,0:T(8,128)S(...) custom-call(s32[256]{0:T(256)S(1)} %copy-done.2, s32[256]{0:T(256)S(1)} %copy-done.3, s32[2]{0:T(128)S(1)} %pad_add_fusion.me, ...), custom_call_target="tpu_custom_call" | custom-call | flops 1000000 | bytes 1048576 | tf_op jit(solution)/shard_map/pallas_call | solution.py:30
  37.3 1.7 %collective-permute-done.11.got = f32[4,8,32,128]{3,2,1,0:T(8,128)S(1)} collective-permute-done((f32[4,8,32,128]{3,2,1,0:T(8,128)S(1)}, f32[4,8,32,128]{3,2,1,0:T(8,128)S(1)}, u32[]{:S(2)}, u32[]{:S(2)}) %collective-permute-start.11) | collective-permute-done | bytes 524320 | tf_op jit(solution)/shard_map/ppermute | solution.py:316
  40.3 2.1 %collective-permute-start.13 = (f32[8,32,128]{2,1,0:T(8,128)S(1)}, f32[8,32,128]{2,1,0:T(8,128)S(1)}, u32[]{:S(2)}, u32[]{:S(2)}) collective-permute-start(f32[8,32,128]{2,1,0:T(8,128)S(1)} %get-tuple-element.90), channel_id=1, source_target_pairs={{0,64},{32,96},{64,0},{96,32},{1,65},{33,97},{65,1},{97,33},{2,66}... | collective-permute-start | bytes 393224 | tf_op jit(solution)/shard_map/ppermute | solution.py:316
  43.0 6.0 %collective-permute-start.22 = (f32[32,8,128]{2,1,0:T(8,128)S(1)}, f32[32,8,128]{2,1,0:T(8,128)S(1)}, u32[]{:S(2)}, u32[]{:S(2)}) collective-permute-start(f32[32,8,128]{2,1,0:T(8,128)S(1)} %get-tuple-element.92), channel_id=1, source_target_pairs={{1,0},{2,1},{3,2},{4,3},{5,4},{6,5},{7,6},{8,7},{9,8},{10,9},{11,1... | collective-permute-start | bytes 393224 | tf_op jit(solution)/shard_map/ppermute | solution.py:386
  49.0 1.4 %collective-permute-start.17 = (f32[8,32,128]{2,1,0:T(8,128)S(1)}, f32[8,32,128]{2,1,0:T(8,128)S(1)}, u32[]{:S(2)}, u32[]{:S(2)}) collective-permute-start(f32[8,32,128]{2,1,0:T(8,128)S(1)} %shard_map.82.refs_0_.sent), channel_id=1, source_target_pairs={{0,32},{32,64},{64,96},{96,0},{1,33},{33,65},{65,97},{97,1},{2,34}... | collective-permute-start | bytes 393224 | tf_op jit(solution)/shard_map/ppermute | solution.py:316
  50.4 2.4 %collective-permute-start.16 = (f32[8,32,128]{2,1,0:T(8,128)S(1)}, f32[8,32,128]{2,1,0:T(8,128)S(1)}, u32[]{:S(2)}, u32[]{:S(2)}) collective-permute-start(f32[8,32,128]{2,1,0:T(8,128)S(1)} %shard_map.82.refs_0_.sent), channel_id=1, source_target_pairs={{0,64},{32,96},{64,0},{96,32},{1,65},{33,97},{65,1},{97,33},{2,66}... | collective-permute-start | bytes 393224 | tf_op jit(solution)/shard_map/ppermute | solution.py:316
  52.9 1.2 %collective-permute-start.23 = (f32[32,8,128]{2,1,0:T(8,128)S(1)}, f32[32,8,128]{2,1,0:T(8,128)S(1)}, u32[]{:S(2)}, u32[]{:S(2)}) collective-permute-start(f32[32,8,128]{2,1,0:T(8,128)S(1)} %get-tuple-element.93), channel_id=1, source_target_pairs={{0,1},{1,2},{2,3},{3,4},{4,5},{5,6},{6,7},{7,8},{8,9},{9,10},{10,1... | collective-permute-start | bytes 393224 | tf_op jit(solution)/shard_map/ppermute | solution.py:386
  54.1 1.8 %collective-permute-start.18 = (f32[8,32,128]{2,1,0:T(8,128)S(1)}, f32[8,32,128]{2,1,0:T(8,128)S(1)}, u32[]{:S(2)}, u32[]{:S(2)}) collective-permute-start(f32[8,32,128]{2,1,0:T(8,128)S(1)} %shard_map.82.refs_0_.sent), channel_id=1, source_target_pairs={{0,16},{16,0},{1,17},{17,1},{2,18},{18,2},{3,19},{19,3},{4,20},{20... | collective-permute-start | bytes 393224 | tf_op jit(solution)/shard_map/ppermute | solution.py:316
  55.9 1.3 %collective-permute-start.21 = (f32[8,32,128]{2,1,0:T(8,128)S(1)}, f32[8,32,128]{2,1,0:T(8,128)S(1)}, u32[]{:S(2)}, u32[]{:S(2)}) collective-permute-start(f32[8,32,128]{2,1,0:T(8,128)S(1)} %collective-permute-done.17.refs_3_), channel_id=1, source_target_pairs={{0,16},{16,0},{1,17},{17,1},{2,18},{18,2},{3,19},{19,3},{4,20},{20... | collective-permute-start | bytes 393224 | tf_op jit(solution)/shard_map/ppermute | solution.py:316
  57.2 1.5 %collective-permute-done.16.refs_2_ = f32[8,32,128]{2,1,0:T(8,128)S(1)} collective-permute-done((f32[8,32,128]{2,1,0:T(8,128)S(1)}, f32[8,32,128]{2,1,0:T(8,128)S(1)}, u32[]{:S(2)}, u32[]{:S(2)}) %collective-permute-start.16) | collective-permute-done | bytes 131104 | tf_op jit(solution)/shard_map/ppermute | solution.py:316
  58.7 1.4 %collective-permute-start.20 = (f32[8,32,128]{2,1,0:T(8,128)S(1)}, f32[8,32,128]{2,1,0:T(8,128)S(1)}, u32[]{:S(2)}, u32[]{:S(2)}) collective-permute-start(f32[8,32,128]{2,1,0:T(8,128)S(1)} %collective-permute-done.16.refs_2_), channel_id=1, source_target_pairs={{0,16},{16,0},{1,17},{17,1},{2,18},{18,2},{3,19},{19,3},{4,20},{20... | collective-permute-start | bytes 393224 | tf_op jit(solution)/shard_map/ppermute | solution.py:316
  61.4 5.4 %shard_map.83 = (f32[4,8,32,128]{3,2,1,0:T(8,128)S(1)}, f32[4,8,32,128]{3,2,1,0:T(8,128)S(1)}, f32[32,32,128]{2,1,0:T(8,128)S(1)}, f32[2,8,128]{2,1,0:T(8,128)S(...) custom-call(s32[256]{0:T(256)S(1)} %copy-done.2, s32[256]{0:T(256)S(1)} %copy-done.3, s32[2]{0:T(128)S(1)} %pad_add_fusion.me, ...), custom_call_target="tpu_custom_call" | custom-call | flops 1000000 | bytes 1048576 | tf_op jit(solution)/shard_map/pallas_call | solution.py:30
  66.9 2.3 %collective-permute-start.24 = (f32[4,8,32,128]{3,2,1,0:T(8,128)S(1)}, f32[4,8,32,128]{3,2,1,0:T(8,128)S(1)}, u32[]{:S(2)}, u32[]{:S(2)}) collective-permute-start(f32[4,8,32,128]{3,2,1,0:T(8,128)S(1)} %get-tuple-element.104), channel_id=1, source_target_pairs={{0,16},{16,0},{1,17},{17,1},{2,18},{18,2},{3,19},{19,3},{4,20},{20... | collective-permute-start | bytes 1572872 | tf_op jit(solution)/shard_map/ppermute | solution.py:316
  69.2 1.5 %collective-permute-done.24.got = f32[4,8,32,128]{3,2,1,0:T(8,128)S(1)} collective-permute-done((f32[4,8,32,128]{3,2,1,0:T(8,128)S(1)}, f32[4,8,32,128]{3,2,1,0:T(8,128)S(1)}, u32[]{:S(2)}, u32[]{:S(2)}) %collective-permute-start.24) | collective-permute-done | bytes 524320 | tf_op jit(solution)/shard_map/ppermute | solution.py:316
  70.8 1.3 %collective-permute-start.25 = (f32[8,32,128]{2,1,0:T(8,128)S(1)}, f32[8,32,128]{2,1,0:T(8,128)S(1)}, u32[]{:S(2)}, u32[]{:S(2)}) collective-permute-start(f32[8,32,128]{2,1,0:T(8,128)S(1)} %get-tuple-element.106), channel_id=1, source_target_pairs={{0,32},{32,64},{64,96},{96,0},{1,33},{33,65},{65,97},{97,1},{2,34}... | collective-permute-start | bytes 393224 | tf_op jit(solution)/shard_map/ppermute | solution.py:316
  72.6 2.0 %collective-permute-start.27 = (f32[8,32,128]{2,1,0:T(8,128)S(1)}, f32[8,32,128]{2,1,0:T(8,128)S(1)}, u32[]{:S(2)}, u32[]{:S(2)}) collective-permute-start(f32[8,32,128]{2,1,0:T(8,128)S(1)} %get-tuple-element.108), channel_id=1, source_target_pairs={{0,96},{32,0},{64,32},{96,64},{1,97},{33,1},{65,33},{97,65},{2,98}... | collective-permute-start | bytes 393224 | tf_op jit(solution)/shard_map/ppermute | solution.py:316
  75.5 1.5 %collective-permute-done.25.a = f32[8,32,128]{2,1,0:T(8,128)S(1)} collective-permute-done((f32[8,32,128]{2,1,0:T(8,128)S(1)}, f32[8,32,128]{2,1,0:T(8,128)S(1)}, u32[]{:S(2)}, u32[]{:S(2)}) %collective-permute-start.25) | collective-permute-done | bytes 131104 | tf_op jit(solution)/shard_map/ppermute | solution.py:316
  77.1 1.6 %collective-permute-done.26.b = f32[8,32,128]{2,1,0:T(8,128)S(1)} collective-permute-done((f32[8,32,128]{2,1,0:T(8,128)S(1)}, f32[8,32,128]{2,1,0:T(8,128)S(1)}, u32[]{:S(2)}, u32[]{:S(2)}) %collective-permute-start.26) | collective-permute-done | bytes 131104 | tf_op jit(solution)/shard_map/ppermute | solution.py:316
  80.8 9.1 %all-to-all-start.1 = ((f32[128,1,128]{2,1,0:T(1,128)}), f32[128,1,128]{2,1,0:T(1,128)S(1)}, u32[]{:S(2)}, u32[]{:S(2)}) async-start(f32[128,1,128]{2,1,0:T(1,128)} %bitcast.9), calls=%async_computation.1 | async-start | bytes 131072 | tf_op jit(solution)/shard_map/all_to_all | solution.py:339
  89.9 5.5 %collective-permute-start.28 = (f32[16,8,128]{2,1,0:T(8,128)S(1)}, f32[16,8,128]{2,1,0:T(8,128)S(1)}, u32[]{:S(2)}, u32[]{:S(2)}) collective-permute-start(f32[16,8,128]{2,1,0:T(8,128)S(1)} %get-tuple-element.123), channel_id=1, source_target_pairs={{1,0},{2,1},{3,2},{4,3},{5,4},{6,5},{7,6},{8,7},{9,8},{10,9},{11,1... | collective-permute-start | bytes 196616 | tf_op jit(solution)/shard_map/ppermute | solution.py:401
  95.4 4.3 %all-to-all-done.1 = f32[128,1,128]{2,1,0:T(1,128)S(1)} async-done(((f32[128,1,128]{2,1,0:T(1,128)}), f32[128,1,128]{2,1,0:T(1,128)S(1)}, u32[]{:S(2)}, u32[]{:S(2)}) %all-to-all-start.1) | async-done | bytes 65568 | tf_op jit(solution)/shard_map/all_to_all | solution.py:339
  101.8 2.7 %shard_map.88 = (f32[32,4096]{1,0:T(8,128)}, f32[32,1024]{1,0:T(8,128)}) custom-call(s32[2]{0:T(128)S(1)} %add_convert_fusion.ends, f32[2]{0:T(128)S(1)} %get-tuple-element.126.alphas, f32[32,4096]{1,0:T(8,128)S(1)} %copy-done, f32[32,32,128]{2,1,0:T(8,128)} %copy-done.4, f32[32,32,128]{2,1,0:T(8,128)S(1)} %get-tuple-element.109.back.turned, ...), custom_call_target="tpu_custom_call" | custom-call | flops 1000000 | bytes 1048576 | tf_op jit(solution)/shard_map/pallas_call | solution.py:30
  (57 shorter events, 14.2 us)
Async XLA Ops:
  6.5 3.0 %collective-permute-start = (f32[4,8,32,128]{3,2,1,0:T(8,128)S(1)}, f32[4,8,32,128]{3,2,1,0:T(8,128)S(1)}, u32[]{:S(2)}, u32[]{:S(2)}) collective-permute-start(f32[4,8,32,128]{3,2,1,0:T(8,128)S(1)} %get-tuple-element.78), channel_id=1, source_target_pairs={{0,16},{16,0},{1,17},{17,1},{2,18},{18,2},{3,19},{19,3},{4,20},{20... | collective-permute-start | bytes 1572872 | tf_op jit(solution)/shard_map/ppermute | solution.py:316
  9.6 6.3 %collective-permute-start.1 = (f32[8,32,128]{2,1,0:T(8,128)S(1)}, f32[8,32,128]{2,1,0:T(8,128)S(1)}, u32[]{:S(2)}, u32[]{:S(2)}) collective-permute-start(f32[8,32,128]{2,1,0:T(8,128)S(1)} %get-tuple-element.80), channel_id=1, source_target_pairs={{0,32},{32,64},{64,96},{96,0},{1,33},{33,65},{65,97},{97,1},{2,34}... | collective-permute-start | bytes 393224 | tf_op jit(solution)/shard_map/ppermute | solution.py:316
  11.0 8.7 %collective-permute-start.2 = (f32[8,32,128]{2,1,0:T(8,128)S(1)}, f32[8,32,128]{2,1,0:T(8,128)S(1)}, u32[]{:S(2)}, u32[]{:S(2)}) collective-permute-start(f32[8,32,128]{2,1,0:T(8,128)S(1)} %get-tuple-element.81), channel_id=1, source_target_pairs={{0,64},{32,96},{64,0},{96,32},{1,65},{33,97},{65,1},{97,33},{2,66}... | collective-permute-start | bytes 393224 | tf_op jit(solution)/shard_map/ppermute | solution.py:316
  13.6 6.0 %collective-permute-start.3 = (f32[8,32,128]{2,1,0:T(8,128)S(1)}, f32[8,32,128]{2,1,0:T(8,128)S(1)}, u32[]{:S(2)}, u32[]{:S(2)}) collective-permute-start(f32[8,32,128]{2,1,0:T(8,128)S(1)} %get-tuple-element.82), channel_id=1, source_target_pairs={{0,96},{32,0},{64,32},{96,64},{1,97},{33,1},{65,33},{97,65},{2,98}... | collective-permute-start | bytes 393224 | tf_op jit(solution)/shard_map/ppermute | solution.py:316
  19.7 6.5 %collective-permute-start.6 = (f32[8,32,128]{2,1,0:T(8,128)S(1)}, f32[8,32,128]{2,1,0:T(8,128)S(1)}, u32[]{:S(2)}, u32[]{:S(2)}) collective-permute-start(f32[8,32,128]{2,1,0:T(8,128)S(1)} %get-tuple-element.83.refs_0_), channel_id=1, source_target_pairs={{0,32},{32,64},{64,96},{96,0},{1,33},{33,65},{65,97},{97,1},{2,34}... | collective-permute-start | bytes 393224 | tf_op jit(solution)/shard_map/ppermute | solution.py:316
  20.8 7.6 %collective-permute-start.5 = (f32[8,32,128]{2,1,0:T(8,128)S(1)}, f32[8,32,128]{2,1,0:T(8,128)S(1)}, u32[]{:S(2)}, u32[]{:S(2)}) collective-permute-start(f32[8,32,128]{2,1,0:T(8,128)S(1)} %get-tuple-element.83.refs_0_), channel_id=1, source_target_pairs={{0,64},{32,96},{64,0},{96,32},{1,65},{33,97},{65,1},{97,33},{2,66}... | collective-permute-start | bytes 393224 | tf_op jit(solution)/shard_map/ppermute | solution.py:316
  23.0 7.3 %collective-permute-start.4 = (f32[8,32,128]{2,1,0:T(8,128)S(1)}, f32[8,32,128]{2,1,0:T(8,128)S(1)}, u32[]{:S(2)}, u32[]{:S(2)}) collective-permute-start(f32[8,32,128]{2,1,0:T(8,128)S(1)} %get-tuple-element.83.refs_0_), channel_id=1, source_target_pairs={{0,96},{32,0},{64,32},{96,64},{1,97},{33,1},{65,33},{97,65},{2,98}... | collective-permute-start | bytes 393224 | tf_op jit(solution)/shard_map/ppermute | solution.py:316
  23.9 6.4 %collective-permute-start.7 = (f32[8,32,128]{2,1,0:T(8,128)S(1)}, f32[8,32,128]{2,1,0:T(8,128)S(1)}, u32[]{:S(2)}, u32[]{:S(2)}) collective-permute-start(f32[8,32,128]{2,1,0:T(8,128)S(1)} %get-tuple-element.83.refs_0_), channel_id=1, source_target_pairs={{0,16},{16,0},{1,17},{17,1},{2,18},{18,2},{3,19},{19,3},{4,20},{20... | collective-permute-start | bytes 393224 | tf_op jit(solution)/shard_map/ppermute | solution.py:316
  26.2 4.1 %collective-permute-start.10 = (f32[8,32,128]{2,1,0:T(8,128)S(1)}, f32[8,32,128]{2,1,0:T(8,128)S(1)}, u32[]{:S(2)}, u32[]{:S(2)}) collective-permute-start(f32[8,32,128]{2,1,0:T(8,128)S(1)} %collective-permute-done.6.refs_3_), channel_id=1, source_target_pairs={{0,16},{16,0},{1,17},{17,1},{2,18},{18,2},{3,19},{19,3},{4,20},{20... | collective-permute-start | bytes 393224 | tf_op jit(solution)/shard_map/ppermute | solution.py:316
  28.4 2.9 %collective-permute-start.9 = (f32[8,32,128]{2,1,0:T(8,128)S(1)}, f32[8,32,128]{2,1,0:T(8,128)S(1)}, u32[]{:S(2)}, u32[]{:S(2)}) collective-permute-start(f32[8,32,128]{2,1,0:T(8,128)S(1)} %collective-permute-done.5.refs_2_), channel_id=1, source_target_pairs={{0,16},{16,0},{1,17},{17,1},{2,18},{18,2},{3,19},{19,3},{4,20},{20... | collective-permute-start | bytes 393224 | tf_op jit(solution)/shard_map/ppermute | solution.py:316
  30.3 1.3 %collective-permute-start.8 = (f32[8,32,128]{2,1,0:T(8,128)S(1)}, f32[8,32,128]{2,1,0:T(8,128)S(1)}, u32[]{:S(2)}, u32[]{:S(2)}) collective-permute-start(f32[8,32,128]{2,1,0:T(8,128)S(1)} %collective-permute-done.4.refs_1_), channel_id=1, source_target_pairs={{0,16},{16,0},{1,17},{17,1},{2,18},{18,2},{3,19},{19,3},{4,20},{20... | collective-permute-start | bytes 393224 | tf_op jit(solution)/shard_map/ppermute | solution.py:316
  37.1 2.0 %collective-permute-start.11 = (f32[4,8,32,128]{3,2,1,0:T(8,128)S(1)}, f32[4,8,32,128]{3,2,1,0:T(8,128)S(1)}, u32[]{:S(2)}, u32[]{:S(2)}) collective-permute-start(f32[4,8,32,128]{3,2,1,0:T(8,128)S(1)} %get-tuple-element.87), channel_id=1, source_target_pairs={{0,16},{16,0},{1,17},{17,1},{2,18},{18,2},{3,19},{19,3},{4,20},{20... | collective-permute-start | bytes 1572872 | tf_op jit(solution)/shard_map/ppermute | solution.py:316
  39.1 9.8 %collective-permute-start.12 = (f32[8,32,128]{2,1,0:T(8,128)S(1)}, f32[8,32,128]{2,1,0:T(8,128)S(1)}, u32[]{:S(2)}, u32[]{:S(2)}) collective-permute-start(f32[8,32,128]{2,1,0:T(8,128)S(1)} %get-tuple-element.89), channel_id=1, source_target_pairs={{0,32},{32,64},{64,96},{96,0},{1,33},{33,65},{65,97},{97,1},{2,34}... | collective-permute-start | bytes 393224 | tf_op jit(solution)/shard_map/ppermute | solution.py:316
  40.3 8.6 %collective-permute-start.13 = (f32[8,32,128]{2,1,0:T(8,128)S(1)}, f32[8,32,128]{2,1,0:T(8,128)S(1)}, u32[]{:S(2)}, u32[]{:S(2)}) collective-permute-start(f32[8,32,128]{2,1,0:T(8,128)S(1)} %get-tuple-element.90), channel_id=1, source_target_pairs={{0,64},{32,96},{64,0},{96,32},{1,65},{33,97},{65,1},{97,33},{2,66}... | collective-permute-start | bytes 393224 | tf_op jit(solution)/shard_map/ppermute | solution.py:316
  42.4 6.5 %collective-permute-start.14 = (f32[8,32,128]{2,1,0:T(8,128)S(1)}, f32[8,32,128]{2,1,0:T(8,128)S(1)}, u32[]{:S(2)}, u32[]{:S(2)}) collective-permute-start(f32[8,32,128]{2,1,0:T(8,128)S(1)} %get-tuple-element.91), channel_id=1, source_target_pairs={{0,96},{32,0},{64,32},{96,64},{1,97},{33,1},{65,33},{97,65},{2,98}... | collective-permute-start | bytes 393224 | tf_op jit(solution)/shard_map/ppermute | solution.py:316
  43.0 11.1 %collective-permute-start.22 = (f32[32,8,128]{2,1,0:T(8,128)S(1)}, f32[32,8,128]{2,1,0:T(8,128)S(1)}, u32[]{:S(2)}, u32[]{:S(2)}) collective-permute-start(f32[32,8,128]{2,1,0:T(8,128)S(1)} %get-tuple-element.92), channel_id=1, source_target_pairs={{1,0},{2,1},{3,2},{4,3},{5,4},{6,5},{7,6},{8,7},{9,8},{10,9},{11,1... | collective-permute-start | bytes 393224 | tf_op jit(solution)/shard_map/ppermute | solution.py:386
  49.0 6.9 %collective-permute-start.17 = (f32[8,32,128]{2,1,0:T(8,128)S(1)}, f32[8,32,128]{2,1,0:T(8,128)S(1)}, u32[]{:S(2)}, u32[]{:S(2)}) collective-permute-start(f32[8,32,128]{2,1,0:T(8,128)S(1)} %shard_map.82.refs_0_.sent), channel_id=1, source_target_pairs={{0,32},{32,64},{64,96},{96,0},{1,33},{33,65},{65,97},{97,1},{2,34}... | collective-permute-start | bytes 393224 | tf_op jit(solution)/shard_map/ppermute | solution.py:316
  50.4 8.2 %collective-permute-start.16 = (f32[8,32,128]{2,1,0:T(8,128)S(1)}, f32[8,32,128]{2,1,0:T(8,128)S(1)}, u32[]{:S(2)}, u32[]{:S(2)}) collective-permute-start(f32[8,32,128]{2,1,0:T(8,128)S(1)} %shard_map.82.refs_0_.sent), channel_id=1, source_target_pairs={{0,64},{32,96},{64,0},{96,32},{1,65},{33,97},{65,1},{97,33},{2,66}... | collective-permute-start | bytes 393224 | tf_op jit(solution)/shard_map/ppermute | solution.py:316
  52.8 7.3 %collective-permute-start.15 = (f32[8,32,128]{2,1,0:T(8,128)S(1)}, f32[8,32,128]{2,1,0:T(8,128)S(1)}, u32[]{:S(2)}, u32[]{:S(2)}) collective-permute-start(f32[8,32,128]{2,1,0:T(8,128)S(1)} %shard_map.82.refs_0_.sent), channel_id=1, source_target_pairs={{0,96},{32,0},{64,32},{96,64},{1,97},{33,1},{65,33},{97,65},{2,98}... | collective-permute-start | bytes 393224 | tf_op jit(solution)/shard_map/ppermute | solution.py:316
  52.9 8.3 %collective-permute-start.23 = (f32[32,8,128]{2,1,0:T(8,128)S(1)}, f32[32,8,128]{2,1,0:T(8,128)S(1)}, u32[]{:S(2)}, u32[]{:S(2)}) collective-permute-start(f32[32,8,128]{2,1,0:T(8,128)S(1)} %get-tuple-element.93), channel_id=1, source_target_pairs={{0,1},{1,2},{2,3},{3,4},{4,5},{5,6},{6,7},{7,8},{8,9},{9,10},{10,1... | collective-permute-start | bytes 393224 | tf_op jit(solution)/shard_map/ppermute | solution.py:386
  54.1 7.1 %collective-permute-start.18 = (f32[8,32,128]{2,1,0:T(8,128)S(1)}, f32[8,32,128]{2,1,0:T(8,128)S(1)}, u32[]{:S(2)}, u32[]{:S(2)}) collective-permute-start(f32[8,32,128]{2,1,0:T(8,128)S(1)} %shard_map.82.refs_0_.sent), channel_id=1, source_target_pairs={{0,16},{16,0},{1,17},{17,1},{2,18},{18,2},{3,19},{19,3},{4,20},{20... | collective-permute-start | bytes 393224 | tf_op jit(solution)/shard_map/ppermute | solution.py:316
  55.9 5.3 %collective-permute-start.21 = (f32[8,32,128]{2,1,0:T(8,128)S(1)}, f32[8,32,128]{2,1,0:T(8,128)S(1)}, u32[]{:S(2)}, u32[]{:S(2)}) collective-permute-start(f32[8,32,128]{2,1,0:T(8,128)S(1)} %collective-permute-done.17.refs_3_), channel_id=1, source_target_pairs={{0,16},{16,0},{1,17},{17,1},{2,18},{18,2},{3,19},{19,3},{4,20},{20... | collective-permute-start | bytes 393224 | tf_op jit(solution)/shard_map/ppermute | solution.py:316
  58.7 2.6 %collective-permute-start.20 = (f32[8,32,128]{2,1,0:T(8,128)S(1)}, f32[8,32,128]{2,1,0:T(8,128)S(1)}, u32[]{:S(2)}, u32[]{:S(2)}) collective-permute-start(f32[8,32,128]{2,1,0:T(8,128)S(1)} %collective-permute-done.16.refs_2_), channel_id=1, source_target_pairs={{0,16},{16,0},{1,17},{17,1},{2,18},{18,2},{3,19},{19,3},{4,20},{20... | collective-permute-start | bytes 393224 | tf_op jit(solution)/shard_map/ppermute | solution.py:316
  60.1 1.3 %collective-permute-start.19 = (f32[8,32,128]{2,1,0:T(8,128)S(1)}, f32[8,32,128]{2,1,0:T(8,128)S(1)}, u32[]{:S(2)}, u32[]{:S(2)}) collective-permute-start(f32[8,32,128]{2,1,0:T(8,128)S(1)} %collective-permute-done.15.refs_1_), channel_id=1, source_target_pairs={{0,16},{16,0},{1,17},{17,1},{2,18},{18,2},{3,19},{19,3},{4,20},{20... | collective-permute-start | bytes 393224 | tf_op jit(solution)/shard_map/ppermute | solution.py:316
  66.9 34.9 %copy-start = (f32[32,4096]{1,0:T(8,128)S(1)}, f32[32,4096]{1,0:T(8,128)}, u32[]{:S(2)}) copy-start(f32[32,4096]{1,0:T(8,128)} %volume.1) | copy-start | bytes 1572868
  66.9 3.8 %collective-permute-start.24 = (f32[4,8,32,128]{3,2,1,0:T(8,128)S(1)}, f32[4,8,32,128]{3,2,1,0:T(8,128)S(1)}, u32[]{:S(2)}, u32[]{:S(2)}) collective-permute-start(f32[4,8,32,128]{3,2,1,0:T(8,128)S(1)} %get-tuple-element.104), channel_id=1, source_target_pairs={{0,16},{16,0},{1,17},{17,1},{2,18},{18,2},{3,19},{19,3},{4,20},{20... | collective-permute-start | bytes 1572872 | tf_op jit(solution)/shard_map/ppermute | solution.py:316
  70.8 6.3 %collective-permute-start.25 = (f32[8,32,128]{2,1,0:T(8,128)S(1)}, f32[8,32,128]{2,1,0:T(8,128)S(1)}, u32[]{:S(2)}, u32[]{:S(2)}) collective-permute-start(f32[8,32,128]{2,1,0:T(8,128)S(1)} %get-tuple-element.106), channel_id=1, source_target_pairs={{0,32},{32,64},{64,96},{96,0},{1,33},{33,65},{65,97},{97,1},{2,34}... | collective-permute-start | bytes 393224 | tf_op jit(solution)/shard_map/ppermute | solution.py:316
  72.1 6.6 %collective-permute-start.26 = (f32[8,32,128]{2,1,0:T(8,128)S(1)}, f32[8,32,128]{2,1,0:T(8,128)S(1)}, u32[]{:S(2)}, u32[]{:S(2)}) collective-permute-start(f32[8,32,128]{2,1,0:T(8,128)S(1)} %get-tuple-element.107), channel_id=1, source_target_pairs={{0,64},{32,96},{64,0},{96,32},{1,65},{33,97},{65,1},{97,33},{2,66}... | collective-permute-start | bytes 393224 | tf_op jit(solution)/shard_map/ppermute | solution.py:316
  72.6 7.2 %collective-permute-start.27 = (f32[8,32,128]{2,1,0:T(8,128)S(1)}, f32[8,32,128]{2,1,0:T(8,128)S(1)}, u32[]{:S(2)}, u32[]{:S(2)}) collective-permute-start(f32[8,32,128]{2,1,0:T(8,128)S(1)} %get-tuple-element.108), channel_id=1, source_target_pairs={{0,96},{32,0},{64,32},{96,64},{1,97},{33,1},{65,33},{97,65},{2,98}... | collective-permute-start | bytes 393224 | tf_op jit(solution)/shard_map/ppermute | solution.py:316
  80.8 18.9 %all-to-all-start.1 = ((f32[128,1,128]{2,1,0:T(1,128)}), f32[128,1,128]{2,1,0:T(1,128)S(1)}, u32[]{:S(2)}, u32[]{:S(2)}) async-start(f32[128,1,128]{2,1,0:T(1,128)} %bitcast.9), calls=%async_computation.1 | async-start | bytes 131072 | tf_op jit(solution)/shard_map/all_to_all | solution.py:339
  89.9 11.2 %collective-permute-start.28 = (f32[16,8,128]{2,1,0:T(8,128)S(1)}, f32[16,8,128]{2,1,0:T(8,128)S(1)}, u32[]{:S(2)}, u32[]{:S(2)}) collective-permute-start(f32[16,8,128]{2,1,0:T(8,128)S(1)} %get-tuple-element.123), channel_id=1, source_target_pairs={{1,0},{2,1},{3,2},{4,3},{5,4},{6,5},{7,6},{8,7},{9,8},{10,9},{11,1... | collective-permute-start | bytes 196616 | tf_op jit(solution)/shard_map/ppermute | solution.py:401
  95.4 6.4 %collective-permute-start.29 = (f32[16,8,128]{2,1,0:T(8,128)S(1)}, f32[16,8,128]{2,1,0:T(8,128)S(1)}, u32[]{:S(2)}, u32[]{:S(2)}) collective-permute-start(f32[16,8,128]{2,1,0:T(8,128)S(1)} %get-tuple-element.124), channel_id=1, source_target_pairs={{0,1},{1,2},{2,3},{3,4},{4,5},{5,6},{6,7},{7,8},{8,9},{9,10},{10,1... | collective-permute-start | bytes 196616 | tf_op jit(solution)/shard_map/ppermute | solution.py:401
  (5 other events, 129.9 us)
